TPU v7x, 256 devices: a whole 4x4x8 slice. The times are simulated.
256 devices in a mesh: gx: 8 (over y_hi, x), gy: 8 (over z), gz: 4 (over y_lo, core).
Axes of the slice: x: 4, y: 4 (y_hi: 2, y_lo: 2; y = y_hi * 2 + y_lo), z: 8, core: 2. Of those that a mesh axis runs over, the one named last changes fastest.
Arguments:
- populations: float32 [39, 64, 192, 512], P(None, 'gx', 'gy', 'gz'), may hold values from 0.5 to 1.5
- relax: float32 [64, 192, 512], P('gx', 'gy', 'gz'), may hold values from 0.6 to 1.9
Outputs:
- advanced: float32 [39, 64, 192, 512], P(None, 'gx', 'gy', 'gz')
All inputs are finite; a program needn't handle non-finite values.
Results may differ from a plain program's by a relative error of at most 0.0001.
Values sent between devices are 32-bit elements; how exact they have to be, the bound alone decides.
A program may use at most 128 MiB of HBM per device.

v0:
```python
import jax
import jax.numpy as jnp
from jax import lax
from jax.sharding import PartitionSpec as P


def from_behind(block, axis, distance):
    devices = range(lax.axis_size(axis))
    route = [((i - distance) % len(devices), i) for i in devices]
    return lax.ppermute(block, axis, route)


def lattice():
    speeds = [(0, 0, 0)]
    weights = [1.0 / 12.0]
    for axis in range(3):
        for sign in (1, -1):
            vector = [0, 0, 0]
            vector[axis] = sign
            speeds.append(tuple(vector))
            weights.append(1.0 / 12.0)
    for first in (1, -1):
        for second in (1, -1):
            for third in (1, -1):
                speeds.append((first, second, third))
                weights.append(1.0 / 27.0)
    for axis in range(3):
        for sign in (2, -2):
            vector = [0, 0, 0]
            vector[axis] = sign
            speeds.append(tuple(vector))
            weights.append(2.0 / 135.0)
    for couple in ((0, 1), (0, 2), (1, 2)):
        for first in (2, -2):
            for second in (2, -2):
                vector = [0, 0, 0]
                vector[couple[0]] = first
                vector[couple[1]] = second
                speeds.append(tuple(vector))
                weights.append(1.0 / 432.0)
    for axis in range(3):
        for sign in (3, -3):
            vector = [0, 0, 0]
            vector[axis] = sign
            speeds.append(tuple(vector))
            weights.append(1.0 / 1620.0)
    return (speeds, weights)


def collide(popul, rate):
    speeds, weights = lattice()
    acoustic_wave_rate = 2.0 / 3.0
    inverse = 1.0 / acoustic_wave_rate**0.5
    zeroth_moment_rho = sum((weights[member] * popul[member] for member in range(39)))
    flux = [
        sum(
            (
                weights[member] * speeds[member][axis] * popul[member]
                for member in range(39)
                if speeds[member][axis] != 0
            )
        )
        for axis in range(3)
    ]
    thermal_heat_content = sum(
        (
            weights[member]
            * float(sum((value * value for value in speeds[member])))
            * popul[member]
            for member in range(1, 39)
        )
    )
    velocity = [part / zeroth_moment_rho for part in flux]
    flow_norm_square = (
        velocity[0] * velocity[0] + velocity[1] * velocity[1] + velocity[2] * velocity[2]
    )
    site_kinetic_heat = (thermal_heat_content / zeroth_moment_rho - flow_norm_square) / (
        3.0 * acoustic_wave_rate
    )
    scaled = [part * inverse for part in velocity]
    scaled_square = flow_norm_square / acoustic_wave_rate
    excess_quantity = site_kinetic_heat - 1.0
    results = []
    for member in range(39):
        vector = speeds[member]
        aligned = (
            sum((vector[axis] * inverse * scaled[axis] for axis in range(3) if vector[axis] != 0))
            if member > 0
            else jnp.zeros_like(zeroth_moment_rho)
        )
        speed_square = float(sum((value * value for value in vector))) / acoustic_wave_rate
        aligned_square = aligned * aligned
        hermite = (
            1.0
            + aligned
            + 0.5 * (aligned_square - scaled_square + excess_quantity * (speed_square - 3.0))
            + aligned
            * (aligned_square - 3.0 * scaled_square + 3.0 * excess_quantity * (speed_square - 5.0))
            / 6.0
            + (
                aligned_square * aligned_square
                - 6.0 * aligned_square * scaled_square
                + 3.0 * scaled_square * scaled_square
                + 6.0
                * excess_quantity
                * (aligned_square * (speed_square - 7.0) + scaled_square * (5.0 - speed_square))
                + 3.0
                * excess_quantity
                * excess_quantity
                * (speed_square * speed_square - 10.0 * speed_square + 15.0)
            )
            / 24.0
        )
        maxwellian_target = zeroth_moment_rho * hermite
        results.append(popul[member] - rate * (popul[member] - maxwellian_target))
    return jnp.stack(results)


def propagate(extended, depth):
    speeds, weights = lattice()
    lengths = [extended.shape[dim] - 2 * depth for dim in (1, 2, 3)]
    results = []
    for member in range(39):
        vector = speeds[member]
        starts = [depth - vector[axis] for axis in range(3)]
        results.append(
            extended[
                member,
                starts[0] : starts[0] + lengths[0],
                starts[1] : starts[1] + lengths[1],
                starts[2] : starts[2] + lengths[2],
            ]
        )
    return jnp.stack(results)


def outbound(full, dim, sign):
    speeds, weights = lattice()
    count = full.shape[dim]
    slabs = []
    for member in range(39):
        speed = speeds[member][dim - 1] * sign
        if speed > 0:
            field = full[member]
            if sign > 0:
                layers = lax.slice_in_dim(field, count - speed, count, axis=dim - 1)
            else:
                layers = lax.slice_in_dim(field, 0, speed, axis=dim - 1)
            slabs.append(jnp.moveaxis(layers, dim - 1, 0))
    return jnp.concatenate(slabs, axis=0)


def empty_layers(field, axis, count):
    shape = list(field.shape)
    shape[axis] = count
    return jnp.zeros(tuple(shape), jnp.float32)


def inbound(full, dim, from_lower, from_upper):
    speeds, weights = lattice()
    axis = dim - 1
    lower_offset = 0
    upper_offset = 0
    layers = []
    for member in range(39):
        field = full[member]
        speed = speeds[member][axis]
        if speed > 0:
            slab = jnp.moveaxis(from_lower[lower_offset : lower_offset + speed], 0, axis)
            lower_offset = lower_offset + speed
            below = jnp.concatenate([empty_layers(field, axis, 3 - speed), slab], axis=axis)
            above = empty_layers(field, axis, 3)
        elif speed < 0:
            slab = jnp.moveaxis(from_upper[upper_offset : upper_offset - speed], 0, axis)
            upper_offset = upper_offset - speed
            below = empty_layers(field, axis, 3)
            above = jnp.concatenate([slab, empty_layers(field, axis, 3 + speed)], axis=axis)
        else:
            below = empty_layers(field, axis, 3)
            above = empty_layers(field, axis, 3)
        layers.append(jnp.concatenate([below, field, above], axis=axis))
    return jnp.stack(layers)


def per_device(populations, relax):
    state = populations
    post = collide(state, relax)
    from_lower = from_behind(outbound(post, 1, 1), "gx", 1)
    from_upper = from_behind(outbound(post, 1, -1), "gx", -1)
    extended = inbound(post, 1, from_lower, from_upper)
    from_lower = from_behind(outbound(extended, 2, 1), "gy", 1)
    from_upper = from_behind(outbound(extended, 2, -1), "gy", -1)
    extended = inbound(extended, 2, from_lower, from_upper)
    from_lower = from_behind(outbound(extended, 3, 1), "gz", 1)
    from_upper = from_behind(outbound(extended, 3, -1), "gz", -1)
    extended = inbound(extended, 3, from_lower, from_upper)
    state = propagate(extended, 3)
    return state


def solution(mesh):
    return jax.shard_map(
        per_device,
        mesh=mesh,
        in_specs=(P(None, "gx", "gy", "gz"), P("gx", "gy", "gz")),
        out_specs=P(None, "gx", "gy", "gz"),
        check_vma=False,
    )
```

profile of v0, /device:TPU:1, one launch (start us, length us, event | category | flops | bytes accessed | tf_op | source)
XLA Modules:
  0.0 104.6 jit_solution(1794607884838969151)
XLA Ops:
  0.0 3.4 %bitcast_subtract_fusion = (f32[8,24,128]{2,1,0:T(8,128)S(1)}, f32[8,24,128]{2,1,0:T(8,128)S(1)}, f32[8,24,128]{2,1,0:T(8,128)S(1)}, f32[8,24,128]{2,1,0:T(8,128...) fusion(f32[8,24,128]{2,1,0:T(8,128)} %param.3, f32[39,8,24,128]{3,2,1,0:T(8,128)} %param.2), kind=kLoop, calls=%fused_computation.549 | loop fusion | flops 7348224 | bytes 4620288 | tf_op jit(solution)/shard_map/sub | solution.py:115
  3.5 1.2 %bitcast_subtract_fusion.4 = (f32[8,24,128]{2,1,0:T(8,128)S(1)}, f32[8,24,128]{2,1,0:T(8,128)S(1)}, f32[8,24,128]{2,1,0:T(8,128)S(1)}, f32[8,24,128]{2,1,0:T(8,1...) fusion(f32[8,24,128]{2,1,0:T(8,128)S(1)} %copy-done.1, ...), kind=kLoop, calls=%fused_computation.572 | loop fusion | flops 9363456 | bytes 3145728 | tf_op jit(solution)/shard_map/sub | solution.py:115
  4.8 1.2 %bitcast_subtract_fusion.12 = (f32[8,24,128]{2,1,0:T(8,128)S(1)}, f32[8,24,128]{2,1,0:T(8,128)S(1)}, f32[8,24,128]{2,1,0:T(8,128)S(1)}, f32[8,24,128]{2,1,0:T(8,...) fusion(f32[8,24,128]{2,1,0:T(8,128)S(1)} %copy-done.1, ...), kind=kLoop, calls=%fused_computation.610 | loop fusion | flops 8945664 | bytes 3047424 | tf_op jit(solution)/shard_map/sub | solution.py:115
  5.9 1.2 %bitcast_subtract_fusion.36 = (f32[8,24,128]{2,1,0:T(8,128)S(1)}, f32[8,24,128]{2,1,0:T(8,128)S(1)}, f32[8,24,128]{2,1,0:T(8,128)S(1)}, f32[8,24,128]{2,1,0:T(8,...) fusion(f32[8,24,128]{2,1,0:T(8,128)S(1)} %copy-done.1, ...), kind=kLoop, calls=%fused_computation.733 | loop fusion | flops 9461760 | bytes 3145728 | tf_op jit(solution)/shard_map/sub | solution.py:115
  7.5 6.0 %collective-permute-start.1 = (f32[18,24,128]{2,1,0:T(8,128)S(1)}, f32[18,24,128]{2,1,0:T(8,128)S(1)}, u32[]{:S(2)}, u32[]{:S(2)}) collective-permute-start(f32[18,24,128]{2,1,0:T(8,128)S(1)} %constant_dynamic-update-slice_fusion.11), channel_id=1, source_target_pairs={{32,0},{64,32},{96,64},{128,96},{160,128},{192,160},{224,192},{0,2... | collective-permute-start | bytes 663560 | tf_op jit(solution)/shard_map/ppermute | solution.py:10
  13.6 0.8 fusion.136
  15.4 0.9 fusion.150
  16.4 0.7 constant_dynamic-update-slice_fusion.60
  18.2 5.0 %collective-permute-done = f32[18,24,128]{2,1,0:T(8,128)S(1)} collective-permute-done((f32[18,24,128]{2,1,0:T(8,128)S(1)}, f32[18,24,128]{2,1,0:T(8,128)S(1)}, u32[]{:S(2)}, u32[]{:S(2)}) %collective-permute-start) | collective-permute-done | bytes 221216 | tf_op jit(solution)/shard_map/ppermute | solution.py:10
  26.4 5.7 %collective-permute-start.3 = (f32[18,14,128]{2,0,1:T(8,128)S(1)}, f32[18,14,128]{2,0,1:T(8,128)}, u32[]{:S(2)}, u32[]{:S(2)}) collective-permute-start(f32[18,14,128]{2,0,1:T(8,128)S(1)} %concatenate.405), channel_id=1, source_target_pairs={{4,0},{8,4},{12,8},{16,12},{20,16},{24,20},{28,24},{0,28},{5,1},{9... | collective-permute-start | bytes 387080 | tf_op jit(solution)/shard_map/ppermute | solution.py:10
  32.0 2.6 %concatenate.391 = f32[18,14,128]{2,0,1:T(8,128)S(1)} concatenate(f32[1,14,128]{2,0,1:T(1,128)} %get-tuple-element.206, f32[1,14,128]{2,0,1:T(1,128)} %get-tuple-element.191, f32[1,14,128]{2,0,1:T(1,128)} %get-tuple-element.186, f32[1,14,128]{2,0,1:T(1,128)} %get-tuple-element.190, f32[1,14,128]{2,0,1:T(1,128)} %get-tuple-element.187, f32[2,14,128]{2,0,1:T(2,128)S(1)} %get-tuple-element.203, ...), dimensions={0} | concatenate | bytes 258048 | tf_op jit(solution)/shard_map/concatenate | solution.py:150
  34.9 1.4 %fusion.87 = (f32[1,14,30,134]{3,2,1,0:T(8,128)}, f32[1,14,30,134]{3,2,1,0:T(8,128)}) fusion(f32[14,30,3]{2,1,0:T(8,128)S(1)} %broadcast.262, f32[14,3,128]{2,1,0:T(4,128)S(1)} %broadcast.263, f32[1,24,128]{2,1,0:T(8,128)S(1)} %broadcast.303, f32[3,24,128]{2,1,0:T(8,128)S(1)} %broadcast.264, f32[2,24,128]{2,1,0:T(8,128)S(1)} %get-tuple-element.124, ...), kind=kLoop, calls=%fused_computation.347 | loop fusion | flops 787920 | bytes 771696 | tf_op jit(solution)/shard_map/stack | solution.py:182
  36.2 1.0 fusion.148
  37.2 1.8 %slice_bitcast_fusion.34 = (f32[14,1,128]{2,1,0:T(1,128)S(1)}, f32[14,1,128]{2,1,0:T(1,128)S(1)}, f32[14,1,128]{2,1,0:T(1,128)S(1)}, f32[14,1,128]{2,1,0:T(1,128)}, f32[14,1,128]{2,1,0:T(1,128)}) fusion(f32[18,14,128]{2,0,1:T(8,128)} %collective-permute-done.3), kind=kLoop, calls=%fused_computation.1191 | loop fusion | bytes 71680 | tf_op jit(solution)/shard_map/transpose | solution.py:174
  39.1 0.9 fusion.114
  41.0 1.1 %fusion.115 = (f32[1,14,30]{0,2,1:T(8,128)}, f32[1,14,30]{0,2,1:T(8,128)}, f32[1,14,30]{0,2,1:T(8,128)}) fusion(f32[14,2,128]{2,1,0:T(2,128)S(1)} %broadcast.302, f32[2,24,128]{2,1,0:T(8,128)S(1)} %broadcast.288, f32[3,24,128]{2,1,0:T(8,128)S(1)} %broadcast.264, f32[14,3,128]{2,1,0:T(4,128)S(1)} %broadcast.263, f32[14,1,128]{2,1,0:T(1,128)S(1)} %get-tuple-element.154, ...), kind=kLoop, calls=%fused_computation.415 | loop fusion | flops 6720 | bytes 436144 | tf_op jit(solution)/shard_map/transpose | solution.py:149
  42.1 1.0 fusion.129
  44.1 1.7 %slice_bitcast_fusion.24 = (f32[14,2,128]{2,1,0:T(2,128)}, f32[14,2,128]{2,1,0:T(2,128)}, f32[14,2,128]{2,1,0:T(2,128)}, f32[14,2,128]{2,1,0:T(2,128)S(1)}, f32[14,2,128]{2,1,0:T(2,128)S(1)}) fusion(f32[18,14,128]{2,0,1:T(8,128)} %collective-permute-done.3), kind=kLoop, calls=%fused_computation.1139 | loop fusion | bytes 143360 | tf_op jit(solution)/shard_map/transpose | solution.py:174
  45.8 0.9 fusion.145
  46.7 2.7 %concatenate.442 = f32[18,14,30]{0,2,1:T(8,128)} concatenate(f32[1,14,30]{0,2,1:T(8,128)} %get-tuple-element.183, f32[1,14,30]{0,2,1:T(8,128)} %get-tuple-element.167, f32[1,14,30]{0,2,1:T(8,128)} %get-tuple-element.168, f32[1,14,30]{0,2,1:T(8,128)} %get-tuple-element.166, f32[1,14,30]{0,2,1:T(8,128)} %get-tuple-element.164, f32[2,14,30]{0,2,1:T(8,128)S(1)} %get-tuple-element.180, ...), dimensions={0} | concatenate | bytes 60480 | tf_op jit(solution)/shard_map/concatenate | solution.py:150
  49.4 3.2 %collective-permute-start.5 = (f32[18,14,30]{0,2,1:T(8,128)}, f32[18,14,30]{0,2,1:T(8,128)S(1)}, u32[]{:S(2)}, u32[]{:S(2)}) collective-permute-start(f32[18,14,30]{0,2,1:T(8,128)} %concatenate.442), channel_id=1, source_target_pairs={{1,0},{2,1},{3,2},{0,3},{5,4},{6,5},{7,6},{4,7},{9,8},{10,9},{11,1... | collective-permute-start | bytes 90728 | tf_op jit(solution)/shard_map/ppermute | solution.py:10
  52.6 1.7 %fusion.108 = (f32[1,14,30]{0,2,1:T(8,128)S(1)}, f32[1,14,30]{0,2,1:T(8,128)}) fusion(f32[14,2,128]{2,1,0:T(2,128)S(1)} %broadcast.302, f32[3,24,128]{2,1,0:T(8,128)S(1)} %broadcast.264, f32[2,24,128]{2,1,0:T(8,128)S(1)} %broadcast.288, f32[14,3,128]{2,1,0:T(4,128)S(1)} %broadcast.263, f32[14,1,128]{2,1,0:T(1,128)} %get-tuple-element.157, ...), kind=kLoop, calls=%fused_computation.408 | loop fusion | flops 5040 | bytes 336160 | tf_op jit(solution)/shard_map/transpose | solution.py:149
  54.3 2.6 %concatenate.424 = f32[18,14,30]{0,2,1:T(8,128)} concatenate(f32[1,14,30]{0,2,1:T(8,128)} %get-tuple-element.184, f32[1,14,30]{0,2,1:T(8,128)} %get-tuple-element.171, f32[1,14,30]{0,2,1:T(8,128)S(1)} %get-tuple-element.170, f32[1,14,30]{0,2,1:T(8,128)} %get-tuple-element.165, f32[1,14,30]{0,2,1:T(8,128)} %get-tuple-element.169, f32[2,14,30]{0,2,1:T(8,128)} %fusion.136, ...), dimensions={0} | concatenate | bytes 60480 | tf_op jit(solution)/shard_map/concatenate | solution.py:150
  57.4 1.5 %fusion.89 = (f32[1,14,30,134]{3,2,1,0:T(8,128)S(1)}, f32[1,14,30,134]{3,2,1,0:T(8,128)S(1)}) fusion(f32[14,30,3]{2,1,0:T(8,128)S(1)} %broadcast.262, f32[14,1,128]{2,1,0:T(1,128)S(1)} %broadcast.305, f32[3,24,128]{2,1,0:T(8,128)S(1)} %broadcast.264, f32[14,3,128]{2,1,0:T(4,128)S(1)} %broadcast.263, f32[14,2,128]{2,1,0:T(2,128)} %get-tuple-element.146, ...), kind=kLoop, calls=%fused_computation.349 | loop fusion | flops 787920 | bytes 746096 | tf_op jit(solution)/shard_map/stack | solution.py:182
  58.9 1.4 %fusion.94 = (f32[1,14,30,134]{3,2,1,0:T(8,128)S(1)}, f32[1,14,30,134]{3,2,1,0:T(8,128)S(1)}) fusion(f32[14,30,3]{2,1,0:T(8,128)S(1)} %broadcast.262, f32[14,1,128]{2,1,0:T(1,128)S(1)} %broadcast.305, f32[1,24,128]{2,1,0:T(8,128)S(1)} %broadcast.303, f32[3,24,128]{2,1,0:T(8,128)S(1)} %broadcast.264, f32[14,3,128]{2,1,0:T(4,128)S(1)} %broadcast.263, ...), kind=kLoop, calls=%fused_computation.354 | loop fusion | flops 900480 | bytes 807536 | tf_op jit(solution)/shard_map/stack | solution.py:182
  60.2 1.4 %fusion.93 = (f32[1,14,30,134]{3,2,1,0:T(8,128)S(1)}, f32[1,14,30,134]{3,2,1,0:T(8,128)S(1)}) fusion(f32[14,30,3]{2,1,0:T(8,128)S(1)} %broadcast.262, f32[14,3,128]{2,1,0:T(4,128)S(1)} %broadcast.263, f32[1,24,128]{2,1,0:T(8,128)S(1)} %broadcast.303, f32[3,24,128]{2,1,0:T(8,128)S(1)} %broadcast.264, f32[14,1,128]{2,1,0:T(1,128)S(1)} %broadcast.305, ...), kind=kLoop, calls=%fused_computation.353 | loop fusion | flops 900480 | bytes 807536 | tf_op jit(solution)/shard_map/stack | solution.py:182
  61.7 0.9 slice_bitcast_fusion.22
  63.1 0.9 slice_bitcast_fusion.23
  65.6 0.7 constant_dynamic-update-slice_fusion.59
  67.3 0.7 constant_dynamic-update-slice_fusion.58
  68.7 0.7 constant_dynamic-update-slice_fusion.57
  70.1 0.7 constant_dynamic-update-slice_fusion.56
  71.6 0.7 constant_dynamic-update-slice_fusion.55
  72.9 0.7 constant_dynamic-update-slice_fusion.54
  74.4 0.7 constant_dynamic-update-slice_fusion.53
  75.9 0.7 constant_dynamic-update-slice_fusion.52
  76.7 0.7 constant_dynamic-update-slice_fusion.51
  77.4 0.7 constant_dynamic-update-slice_fusion.50
  78.1 0.7 constant_dynamic-update-slice_fusion.49
  78.9 0.7 constant_dynamic-update-slice_fusion.48
  79.6 0.7 constant_dynamic-update-slice_fusion.47
  80.3 0.7 constant_dynamic-update-slice_fusion.46
  81.1 1.7 %constant_dynamic-update-slice_fusion.45 = f32[39,8,24,128]{3,2,1,0:T(8,128)} fusion(f32[39,8,24,128]{3,2,1,0:T(8,128)} %constant_dynamic-update-slice_fusion.46, f32[1,14,30,134]{3,2,1,0:T(8,128)} %get-tuple-element.93), kind=kLoop, calls=%fused_computation.533 | loop fusion | bytes 196608
  82.7 1.7 %constant_dynamic-update-slice_fusion.44 = f32[39,8,24,128]{3,2,1,0:T(8,128)} fusion(f32[39,8,24,128]{3,2,1,0:T(8,128)} %constant_dynamic-update-slice_fusion.45, f32[1,14,30,134]{3,2,1,0:T(8,128)} %get-tuple-element.92), kind=kLoop, calls=%fused_computation.532 | loop fusion | bytes 196608
  84.4 0.7 constant_dynamic-update-slice_fusion.43
  85.2 0.7 constant_dynamic-update-slice_fusion.42
  87.3 0.7 constant_dynamic-update-slice_fusion.41
  88.1 0.7 constant_dynamic-update-slice_fusion.40
  88.8 0.7 constant_dynamic-update-slice_fusion.39
  89.5 0.7 constant_dynamic-update-slice_fusion.38
  90.3 0.7 constant_dynamic-update-slice_fusion.37
  91.0 0.7 constant_dynamic-update-slice_fusion.36
  92.4 0.7 constant_dynamic-update-slice_fusion.35
  93.7 0.7 constant_dynamic-update-slice_fusion.34
  94.4 0.7 constant_dynamic-update-slice_fusion.33
  95.2 0.7 constant_dynamic-update-slice_fusion.32
  95.9 0.8 fusion.98
  96.7 0.7 constant_dynamic-update-slice_fusion.31
  98.1 0.7 constant_dynamic-update-slice_fusion.30
  98.8 0.7 constant_dynamic-update-slice_fusion.29
  99.5 0.7 constant_dynamic-update-slice_fusion.28
  101.0 0.7 constant_dynamic-update-slice_fusion.26
  102.5 0.7 constant_dynamic-update-slice_fusion.24
  103.9 0.7 constant_dynamic-update-slice_fusion.22
  (243 shorter events, 20.1 us)
Async XLA Ops:
  3.4 12.0 %copy-start.22 = (f32[8,24,128]{2,1,0:T(8,128)}, f32[8,24,128]{2,1,0:T(8,128)S(1)}, u32[]{:S(2)}) copy-start(f32[8,24,128]{2,1,0:T(8,128)S(1)} %get-tuple-element.5) | copy-start | bytes 294916
  4.7 9.8 %copy-start.30 = (f32[8,24,128]{2,1,0:T(8,128)}, f32[8,24,128]{2,1,0:T(8,128)S(1)}, u32[]{:S(2)}) copy-start(f32[8,24,128]{2,1,0:T(8,128)S(1)} %get-tuple-element.64) | copy-start | bytes 294916
  4.7 10.1 %copy-start.8 = (f32[8,24,128]{2,1,0:T(8,128)}, f32[8,24,128]{2,1,0:T(8,128)S(1)}, u32[]{:S(2)}) copy-start(f32[8,24,128]{2,1,0:T(8,128)S(1)} %get-tuple-element.56) | copy-start | bytes 294916
  4.7 10.1 %copy-start.10 = (f32[8,24,128]{2,1,0:T(8,128)}, f32[8,24,128]{2,1,0:T(8,128)S(1)}, u32[]{:S(2)}) copy-start(f32[8,24,128]{2,1,0:T(8,128)S(1)} %get-tuple-element.53) | copy-start | bytes 294916
  4.7 11.6 %copy-start.6 = (f32[8,24,128]{2,1,0:T(8,128)}, f32[8,24,128]{2,1,0:T(8,128)S(1)}, u32[]{:S(2)}) copy-start(f32[8,24,128]{2,1,0:T(8,128)S(1)} %get-tuple-element.54) | copy-start | bytes 294916
  4.7 11.6 %copy-start.7 = (f32[8,24,128]{2,1,0:T(8,128)}, f32[8,24,128]{2,1,0:T(8,128)S(1)}, u32[]{:S(2)}) copy-start(f32[8,24,128]{2,1,0:T(8,128)S(1)} %get-tuple-element.57) | copy-start | bytes 294916
  4.7 19.2 %copy-start.14 = (f32[8,24,128]{2,1,0:T(8,128)}, f32[8,24,128]{2,1,0:T(8,128)S(1)}, u32[]{:S(2)}) copy-start(f32[8,24,128]{2,1,0:T(8,128)S(1)} %get-tuple-element.55) | copy-start | bytes 294916
  4.7 19.8 %copy-start.18 = (f32[8,24,128]{2,1,0:T(8,128)}, f32[8,24,128]{2,1,0:T(8,128)S(1)}, u32[]{:S(2)}) copy-start(f32[8,24,128]{2,1,0:T(8,128)S(1)} %get-tuple-element.58) | copy-start | bytes 294916
  7.2 16.7 %copy-start.4 = (f32[8,24,128]{2,1,0:T(8,128)}, f32[8,24,128]{2,1,0:T(8,128)S(1)}, u32[]{:S(2)}) copy-start(f32[8,24,128]{2,1,0:T(8,128)S(1)} %get-tuple-element.43) | copy-start | bytes 294916
  7.2 18.1 %copy-start.20 = (f32[8,24,128]{2,1,0:T(8,128)}, f32[8,24,128]{2,1,0:T(8,128)S(1)}, u32[]{:S(2)}) copy-start(f32[8,24,128]{2,1,0:T(8,128)S(1)} %get-tuple-element.42) | copy-start | bytes 294916
  7.2 18.1 %copy-start.24 = (f32[8,24,128]{2,1,0:T(8,128)}, f32[8,24,128]{2,1,0:T(8,128)S(1)}, u32[]{:S(2)}) copy-start(f32[8,24,128]{2,1,0:T(8,128)S(1)} %get-tuple-element.49) | copy-start | bytes 294916
  7.2 18.1 %copy-start.26 = (f32[8,24,128]{2,1,0:T(8,128)}, f32[8,24,128]{2,1,0:T(8,128)S(1)}, u32[]{:S(2)}) copy-start(f32[8,24,128]{2,1,0:T(8,128)S(1)} %get-tuple-element.52) | copy-start | bytes 294916
  7.2 18.7 %copy-start.28 = (f32[8,24,128]{2,1,0:T(8,128)}, f32[8,24,128]{2,1,0:T(8,128)S(1)}, u32[]{:S(2)}) copy-start(f32[8,24,128]{2,1,0:T(8,128)S(1)} %get-tuple-element.51) | copy-start | bytes 294916
  7.2 33.8 %copy-start.12 = (f32[8,24,128]{2,1,0:T(8,128)}, f32[8,24,128]{2,1,0:T(8,128)S(1)}, u32[]{:S(2)}) copy-start(f32[8,24,128]{2,1,0:T(8,128)S(1)} %get-tuple-element.41) | copy-start | bytes 294916
  7.2 34.8 %copy-start.16 = (f32[8,24,128]{2,1,0:T(8,128)}, f32[8,24,128]{2,1,0:T(8,128)S(1)}, u32[]{:S(2)}) copy-start(f32[8,24,128]{2,1,0:T(8,128)S(1)} %get-tuple-element.44) | copy-start | bytes 294916
  7.2 36.6 %copy-start.2 = (f32[8,24,128]{2,1,0:T(8,128)}, f32[8,24,128]{2,1,0:T(8,128)S(1)}, u32[]{:S(2)}) copy-start(f32[8,24,128]{2,1,0:T(8,128)S(1)} %get-tuple-element.40) | copy-start | bytes 294916
  7.5 10.1 %collective-permute-start.1 = (f32[18,24,128]{2,1,0:T(8,128)S(1)}, f32[18,24,128]{2,1,0:T(8,128)S(1)}, u32[]{:S(2)}, u32[]{:S(2)}) collective-permute-start(f32[18,24,128]{2,1,0:T(8,128)S(1)} %constant_dynamic-update-slice_fusion.11), channel_id=1, source_target_pairs={{32,0},{64,32},{96,64},{128,96},{160,128},{192,160},{224,192},{0,2... | collective-permute-start | bytes 663560 | tf_op jit(solution)/shard_map/ppermute | solution.py:10
  13.5 9.7 %collective-permute-start = (f32[18,24,128]{2,1,0:T(8,128)S(1)}, f32[18,24,128]{2,1,0:T(8,128)S(1)}, u32[]{:S(2)}, u32[]{:S(2)}) collective-permute-start(f32[18,24,128]{2,1,0:T(8,128)S(1)} %constant_dynamic-update-slice_fusion), channel_id=1, source_target_pairs={{224,0},{0,32},{32,64},{64,96},{96,128},{128,160},{160,192},{192,2... | collective-permute-start | bytes 663560 | tf_op jit(solution)/shard_map/ppermute | solution.py:10
  15.4 16.6 %copy-start.62 = (f32[3,14,128]{2,0,1:T(4,128)S(1)}, f32[3,14,128]{2,0,1:T(4,128)}, u32[]{:S(2)}) copy-start(f32[3,14,128]{2,0,1:T(4,128)} %get-tuple-element.198) | copy-start | bytes 64516
  17.6 8.4 %copy-start.34 = (f32[18,24,128]{2,1,0:T(8,128)}, f32[18,24,128]{2,1,0:T(8,128)S(1)}, u32[]{:S(2)}) copy-start(f32[18,24,128]{2,1,0:T(8,128)S(1)} %collective-permute-done.1) | copy-start | bytes 663556
  18.2 23.8 %copy-start.40 = (f32[1,24,128]{2,1,0:T(8,128)}, f32[1,24,128]{2,1,0:T(8,128)S(1)}, u32[]{:S(2)}) copy-start(f32[1,24,128]{2,1,0:T(8,128)S(1)} %get-tuple-element.134) | copy-start | bytes 36868
  18.2 23.8 %copy-start.42 = (f32[1,24,128]{2,1,0:T(8,128)}, f32[1,24,128]{2,1,0:T(8,128)S(1)}, u32[]{:S(2)}) copy-start(f32[1,24,128]{2,1,0:T(8,128)S(1)} %get-tuple-element.137) | copy-start | bytes 36868
  18.2 23.8 %copy-start.48 = (f32[1,24,128]{2,1,0:T(8,128)}, f32[1,24,128]{2,1,0:T(8,128)S(1)}, u32[]{:S(2)}) copy-start(f32[1,24,128]{2,1,0:T(8,128)S(1)} %get-tuple-element.135) | copy-start | bytes 36868
  18.2 23.8 %copy-start.44 = (f32[1,24,128]{2,1,0:T(8,128)}, f32[1,24,128]{2,1,0:T(8,128)S(1)}, u32[]{:S(2)}) copy-start(f32[1,24,128]{2,1,0:T(8,128)S(1)} %get-tuple-element.136) | copy-start | bytes 36868
  23.9 18.2 %copy-start.50 = (f32[1,24,128]{2,1,0:T(8,128)}, f32[1,24,128]{2,1,0:T(8,128)S(1)}, u32[]{:S(2)}) copy-start(f32[1,24,128]{2,1,0:T(8,128)S(1)} %get-tuple-element.139) | copy-start | bytes 36868
  25.2 18.5 %copy-start.36 = (f32[2,24,128]{2,1,0:T(8,128)}, f32[2,24,128]{2,1,0:T(8,128)S(1)}, u32[]{:S(2)}) copy-start(f32[2,24,128]{2,1,0:T(8,128)S(1)} %get-tuple-element.128) | copy-start | bytes 73732
  25.2 18.5 %copy-start.38 = (f32[2,24,128]{2,1,0:T(8,128)}, f32[2,24,128]{2,1,0:T(8,128)S(1)}, u32[]{:S(2)}) copy-start(f32[2,24,128]{2,1,0:T(8,128)S(1)} %get-tuple-element.127) | copy-start | bytes 73732
  25.2 13.9 %copy-start.39 = (f32[2,24,128]{2,1,0:T(8,128)}, f32[2,24,128]{2,1,0:T(8,128)S(1)}, u32[]{:S(2)}) copy-start(f32[2,24,128]{2,1,0:T(8,128)S(1)} %get-tuple-element.133) | copy-start | bytes 73732
  25.2 18.5 %copy-start.32 = (f32[2,24,128]{2,1,0:T(8,128)}, f32[2,24,128]{2,1,0:T(8,128)S(1)}, u32[]{:S(2)}) copy-start(f32[2,24,128]{2,1,0:T(8,128)S(1)} %get-tuple-element.131) | copy-start | bytes 73732
  25.2 18.9 %copy-start.37 = (f32[2,24,128]{2,1,0:T(8,128)}, f32[2,24,128]{2,1,0:T(8,128)S(1)}, u32[]{:S(2)}) copy-start(f32[2,24,128]{2,1,0:T(8,128)S(1)} %get-tuple-element.132) | copy-start | bytes 73732
  26.4 10.9 %collective-permute-start.3 = (f32[18,14,128]{2,0,1:T(8,128)S(1)}, f32[18,14,128]{2,0,1:T(8,128)}, u32[]{:S(2)}, u32[]{:S(2)}) collective-permute-start(f32[18,14,128]{2,0,1:T(8,128)S(1)} %concatenate.405), channel_id=1, source_target_pairs={{4,0},{8,4},{12,8},{16,12},{20,16},{24,20},{28,24},{0,28},{5,1},{9... | collective-permute-start | bytes 387080 | tf_op jit(solution)/shard_map/ppermute | solution.py:10
  34.6 5.7 %collective-permute-start.2 = (f32[18,14,128]{2,0,1:T(8,128)S(1)}, f32[18,14,128]{2,0,1:T(8,128)S(1)}, u32[]{:S(2)}, u32[]{:S(2)}) collective-permute-start(f32[18,14,128]{2,0,1:T(8,128)S(1)} %concatenate.391), channel_id=1, source_target_pairs={{28,0},{0,4},{4,8},{8,12},{12,16},{16,20},{20,24},{24,28},{29,1},{... | collective-permute-start | bytes 387080 | tf_op jit(solution)/shard_map/ppermute | solution.py:10
  39.1 4.7 %copy-start.69 = (f32[14,1,128]{2,1,0:T(1,128)}, f32[14,1,128]{2,1,0:T(1,128)S(1)}, u32[]{:S(2)}) copy-start(f32[14,1,128]{2,1,0:T(1,128)S(1)} %get-tuple-element.156) | copy-start | bytes 21508
  39.1 4.7 %copy-start.71 = (f32[14,1,128]{2,1,0:T(1,128)}, f32[14,1,128]{2,1,0:T(1,128)S(1)}, u32[]{:S(2)}) copy-start(f32[14,1,128]{2,1,0:T(1,128)S(1)} %get-tuple-element.155) | copy-start | bytes 21508
  39.1 4.7 %copy-start.76 = (f32[14,1,128]{2,1,0:T(1,128)}, f32[14,1,128]{2,1,0:T(1,128)S(1)}, u32[]{:S(2)}) copy-start(f32[14,1,128]{2,1,0:T(1,128)S(1)} %get-tuple-element.154) | copy-start | bytes 21508
  49.4 15.1 %collective-permute-start.5 = (f32[18,14,30]{0,2,1:T(8,128)}, f32[18,14,30]{0,2,1:T(8,128)S(1)}, u32[]{:S(2)}, u32[]{:S(2)}) collective-permute-start(f32[18,14,30]{0,2,1:T(8,128)} %concatenate.442), channel_id=1, source_target_pairs={{1,0},{2,1},{3,2},{0,3},{5,4},{6,5},{7,6},{4,7},{9,8},{10,9},{11,1... | collective-permute-start | bytes 90728 | tf_op jit(solution)/shard_map/ppermute | solution.py:10
  56.9 5.6 %copy-start.11 = (f32[8,24,128]{2,1,0:T(8,128)S(1)}, f32[8,24,128]{2,1,0:T(8,128)}, u32[]{:S(2)}) copy-start(f32[8,24,128]{2,1,0:T(8,128)} %copy-done.10) | copy-start | bytes 294916
  56.9 5.6 %copy-start.27 = (f32[8,24,128]{2,1,0:T(8,128)S(1)}, f32[8,24,128]{2,1,0:T(8,128)}, u32[]{:S(2)}) copy-start(f32[8,24,128]{2,1,0:T(8,128)} %copy-done.26) | copy-start | bytes 294916
  57.0 5.7 %slice-start.1 = ((f32[18,24,128]{2,1,0:T(8,128)}), f32[3,24,128]{2,1,0:T(8,128)S(1)}, s32[]{:S(2)}) async-start(f32[18,24,128]{2,1,0:T(8,128)} %copy-done.35), calls=%async_computation.1 | async-start | bytes 73728 | tf_op jit(solution)/shard_map/slice | solution.py:169
  57.0 7.0 %copy-start.9 = (f32[8,24,128]{2,1,0:T(8,128)S(1)}, f32[8,24,128]{2,1,0:T(8,128)}, u32[]{:S(2)}) copy-start(f32[8,24,128]{2,1,0:T(8,128)} %copy-done.8) | copy-start | bytes 294916
  57.0 7.0 %copy-start.25 = (f32[8,24,128]{2,1,0:T(8,128)S(1)}, f32[8,24,128]{2,1,0:T(8,128)}, u32[]{:S(2)}) copy-start(f32[8,24,128]{2,1,0:T(8,128)} %copy-done.24) | copy-start | bytes 294916
  57.0 7.0 %slice-start = ((f32[18,24,128]{2,1,0:T(8,128)}), f32[3,24,128]{2,1,0:T(8,128)S(1)}, s32[]{:S(2)}) async-start(f32[18,24,128]{2,1,0:T(8,128)} %copy-done.34), calls=%async_computation | async-start | bytes 73728 | tf_op jit(solution)/shard_map/slice | solution.py:174
  57.0 9.3 %collective-permute-start.4 = (f32[18,14,30]{0,2,1:T(8,128)}, f32[18,14,30]{0,2,1:T(8,128)S(1)}, u32[]{:S(2)}, u32[]{:S(2)}) collective-permute-start(f32[18,14,30]{0,2,1:T(8,128)} %concatenate.424), channel_id=1, source_target_pairs={{3,0},{0,1},{1,2},{2,3},{7,4},{4,5},{5,6},{6,7},{11,8},{8,9},{9,10... | collective-permute-start | bytes 90728 | tf_op jit(solution)/shard_map/ppermute | solution.py:10
  60.2 4.6 %copy-start.31 = (f32[8,24,128]{2,1,0:T(8,128)S(1)}, f32[8,24,128]{2,1,0:T(8,128)}, u32[]{:S(2)}) copy-start(f32[8,24,128]{2,1,0:T(8,128)} %copy-done.30) | copy-start | bytes 294916
  60.2 4.6 %copy-start.45 = (f32[1,24,128]{2,1,0:T(8,128)S(1)}, f32[1,24,128]{2,1,0:T(8,128)}, u32[]{:S(2)}) copy-start(f32[1,24,128]{2,1,0:T(8,128)} %copy-done.44) | copy-start | bytes 36868
  60.2 4.6 %copy-start.67 = (f32[14,1,128]{2,1,0:T(1,128)S(1)}, f32[14,1,128]{2,1,0:T(1,128)}, u32[]{:S(2)}) copy-start(f32[14,1,128]{2,1,0:T(1,128)} %copy-done.66) | copy-start | bytes 21508
  60.2 4.6 %copy-start.79 = (f32[1,24,128]{2,1,0:T(8,128)S(1)}, f32[1,24,128]{2,1,0:T(8,128)}, u32[]{:S(2)}) copy-start(f32[1,24,128]{2,1,0:T(8,128)} %get-tuple-element.143) | copy-start | bytes 36868
  66.3 4.5 %copy-start.17 = (f32[8,24,128]{2,1,0:T(8,128)S(1)}, f32[8,24,128]{2,1,0:T(8,128)}, u32[]{:S(2)}) copy-start(f32[8,24,128]{2,1,0:T(8,128)} %copy-done.16) | copy-start | bytes 294916
  66.3 4.5 %copy-start.49 = (f32[1,24,128]{2,1,0:T(8,128)S(1)}, f32[1,24,128]{2,1,0:T(8,128)}, u32[]{:S(2)}) copy-start(f32[1,24,128]{2,1,0:T(8,128)} %copy-done.48) | copy-start | bytes 36868
  66.3 4.5 %copy-start.70 = (f32[14,1,128]{2,1,0:T(1,128)S(1)}, f32[14,1,128]{2,1,0:T(1,128)}, u32[]{:S(2)}) copy-start(f32[14,1,128]{2,1,0:T(1,128)} %copy-done.69) | copy-start | bytes 21508
  67.3 5.0 %copy-start.13 = (f32[8,24,128]{2,1,0:T(8,128)S(1)}, f32[8,24,128]{2,1,0:T(8,128)}, u32[]{:S(2)}) copy-start(f32[8,24,128]{2,1,0:T(8,128)} %copy-done.12) | copy-start | bytes 294916
  67.3 5.0 %copy-start.41 = (f32[1,24,128]{2,1,0:T(8,128)S(1)}, f32[1,24,128]{2,1,0:T(8,128)}, u32[]{:S(2)}) copy-start(f32[1,24,128]{2,1,0:T(8,128)} %copy-done.40) | copy-start | bytes 36868
  67.3 5.0 %copy-start.77 = (f32[14,1,128]{2,1,0:T(1,128)S(1)}, f32[14,1,128]{2,1,0:T(1,128)}, u32[]{:S(2)}) copy-start(f32[14,1,128]{2,1,0:T(1,128)} %copy-done.76) | copy-start | bytes 21508
  68.7 5.0 %copy-start.21 = (f32[8,24,128]{2,1,0:T(8,128)S(1)}, f32[8,24,128]{2,1,0:T(8,128)}, u32[]{:S(2)}) copy-start(f32[8,24,128]{2,1,0:T(8,128)} %copy-done.20) | copy-start | bytes 294916
  68.7 5.0 %copy-start.47 = (f32[1,24,128]{2,1,0:T(8,128)S(1)}, f32[1,24,128]{2,1,0:T(8,128)}, u32[]{:S(2)}) copy-start(f32[1,24,128]{2,1,0:T(8,128)} %copy-done.46) | copy-start | bytes 36868
  68.7 5.0 %copy-start.68 = (f32[14,1,128]{2,1,0:T(1,128)S(1)}, f32[14,1,128]{2,1,0:T(1,128)}, u32[]{:S(2)}) copy-start(f32[14,1,128]{2,1,0:T(1,128)} %get-tuple-element.162) | copy-start | bytes 21508
  70.8 4.4 %copy-start.75 = (f32[14,1,128]{2,1,0:T(1,128)S(1)}, f32[14,1,128]{2,1,0:T(1,128)}, u32[]{:S(2)}) copy-start(f32[14,1,128]{2,1,0:T(1,128)} %copy-done.74) | copy-start | bytes 21508
  75.9 10.8 %copy-start.3 = (f32[8,24,128]{2,1,0:T(8,128)S(1)}, f32[8,24,128]{2,1,0:T(8,128)}, u32[]{:S(2)}) copy-start(f32[8,24,128]{2,1,0:T(8,128)} %copy-done.2) | copy-start | bytes 294916
  75.9 10.8 %copy-start.5 = (f32[8,24,128]{2,1,0:T(8,128)S(1)}, f32[8,24,128]{2,1,0:T(8,128)}, u32[]{:S(2)}) copy-start(f32[8,24,128]{2,1,0:T(8,128)} %copy-done.4) | copy-start | bytes 294916
  85.9 5.8 %copy-start.33 = (f32[2,24,128]{2,1,0:T(8,128)S(1)}, f32[2,24,128]{2,1,0:T(8,128)}, u32[]{:S(2)}) copy-start(f32[2,24,128]{2,1,0:T(8,128)} %copy-done.32) | copy-start | bytes 73732
  86.7 9.2 %copy-start.59 = (f32[14,2,128]{2,1,0:T(2,128)S(1)}, f32[14,2,128]{2,1,0:T(2,128)}, u32[]{:S(2)}) copy-start(f32[14,2,128]{2,1,0:T(2,128)} %copy-done.58) | copy-start | bytes 43012
  86.7 9.2 %copy-start.61 = (f32[14,2,128]{2,1,0:T(2,128)S(1)}, f32[14,2,128]{2,1,0:T(2,128)}, u32[]{:S(2)}) copy-start(f32[14,2,128]{2,1,0:T(2,128)} %copy-done.60) | copy-start | bytes 43012
  91.0 6.4 %copy-start.55 = (f32[14,2,128]{2,1,0:T(2,128)S(1)}, f32[14,2,128]{2,1,0:T(2,128)}, u32[]{:S(2)}) copy-start(f32[14,2,128]{2,1,0:T(2,128)} %copy-done.54) | copy-start | bytes 43012
  91.0 6.4 %copy-start.57 = (f32[14,2,128]{2,1,0:T(2,128)S(1)}, f32[14,2,128]{2,1,0:T(2,128)}, u32[]{:S(2)}) copy-start(f32[14,2,128]{2,1,0:T(2,128)} %copy-done.56) | copy-start | bytes 43012
  (26 other events, 68.8 us)
where the time goes:
time: 105 us
  local copies, waits for them, and re-layouts  48.8 us (46%)
  other arithmetic  33.1 us (32%)
  starting transfers between devices  15.6 us (15%)
  waiting for transfers between devices  5.73 us (5%)
  between operations  1.3 us (1%)
    unnamed x221, local copies, waits for them, and re-layouts  30.2 us
    ppermute x6, starting transfers between devices, from_behind(): return lax.ppermute(block, axis, route)  15.6 us
    another operation x20, other arithmetic, inbound(): return jnp.stack(layers)  15 us
    transpose x14, other arithmetic, outbound(): slabs.append(jnp.moveaxis(layers, dim - 1, 0))  11.1 us
    concatenate x6, local copies, waits for them, and re-layouts, outbound(): return jnp.concatenate(slabs, axis=0)  8.28 us
    sub x4, other arithmetic, collide(): results.append(popul[member] - rate * (popul[member] - maxwellian_target))  7.04 us
    ppermute x6, waiting for transfers between devices, from_behind(): return lax.ppermute(block, axis, route)  5.73 us
    transpose x6, local copies, waits for them, and re-layouts, inbound(): slab = jnp.moveaxis(from_upper[upper_offset:upper_offset - speed], 0, axis)  5.21 us
  transfers between devices with their start and end apart: 6, of which 3 were waited for; matrix products, arithmetic and copies ran while one was open for 24% of the time, Pallas kernels for 0%

commit v1 on v0

v1 whole, which is shorter than its diff:
```python
import functools

import jax
import jax.numpy as jnp
from jax import lax
from jax.experimental import pallas as pl
from jax.experimental.pallas import tpu as pltpu
from jax.sharding import PartitionSpec as P

MESH = pl.DeviceIdType.MESH
F32 = jnp.float32


def lattice():
    speeds = [(0, 0, 0)]
    weights = [1.0 / 12.0]
    for axis in range(3):
        for sign in (1, -1):
            vector = [0, 0, 0]
            vector[axis] = sign
            speeds.append(tuple(vector))
            weights.append(1.0 / 12.0)
    for first in (1, -1):
        for second in (1, -1):
            for third in (1, -1):
                speeds.append((first, second, third))
                weights.append(1.0 / 27.0)
    for axis in range(3):
        for sign in (2, -2):
            vector = [0, 0, 0]
            vector[axis] = sign
            speeds.append(tuple(vector))
            weights.append(2.0 / 135.0)
    for couple in ((0, 1), (0, 2), (1, 2)):
        for first in (2, -2):
            for second in (2, -2):
                vector = [0, 0, 0]
                vector[couple[0]] = first
                vector[couple[1]] = second
                speeds.append(tuple(vector))
                weights.append(1.0 / 432.0)
    for axis in range(3):
        for sign in (3, -3):
            vector = [0, 0, 0]
            vector[axis] = sign
            speeds.append(tuple(vector))
            weights.append(1.0 / 1620.0)
    return speeds, weights


SPEEDS, WEIGHTS = lattice()
Q = 39
INDEX = {vector: member for member, vector in enumerate(SPEEDS)}
ROWS = 32


def slots(axis, sign):
    table, offset = {}, 0
    for member in range(Q):
        speed = SPEEDS[member][axis] * sign
        if speed > 0:
            table[member] = offset
            offset += speed
    return table


XS = {sign: slots(0, sign) for sign in (1, -1)}
YS = {sign: slots(1, sign) for sign in (1, -1)}
ZS = {sign: slots(2, sign) for sign in (1, -1)}
EARLY = {sign: [m for m in XS[sign] if SPEEDS[m][2] == 0 and abs(SPEEDS[m][0]) < 3] for sign in (1, -1)}
THIRD = {sign: [m for m in XS[sign] if abs(SPEEDS[m][0]) == 3] for sign in (1, -1)}
LATE = {sign: [m for m in XS[sign] if SPEEDS[m][2] != 0] for sign in (1, -1)}
CORNERS = [(1, 1), (1, -1), (-1, 1), (-1, -1)]
SHELLS = {0.0: "0", 1.0: "1", 3.0: "c", 4.0: "2", 8.0: "e", 9.0: "3"}


def square(member):
    return float(sum(value * value for value in SPEEDS[member]))


def final_row(member):
    return 8 if SPEEDS[member][1] < 0 else 0


def corner_rows(sx, sy):
    rows = []
    for member in range(Q):
        cx, cy = SPEEDS[member][0] * sx, SPEEDS[member][1] * sy
        if cx > 0 and cy > 0:
            rows += [(member, layer, row) for layer in range(cx) for row in range(cy)]
    return rows


def leaving_row(member, row, ny):
    cy = SPEEDS[member][1]
    return ny + row if cy > 0 else 8 + cy + row


def entering_row(member, row, ny):
    cy = SPEEDS[member][1]
    return row if cy > 0 else 8 + ny + cy + row


def strided(ref, member, row):
    count, layers, rows, lanes = ref.shape
    return ref.reshape(count * layers * rows, lanes), pl.ds(member * layers * rows + row, layers, stride=rows)


def read_rows(ref, member, row):
    flat, where = strided(ref, member, row)
    return flat[where, :]


def write_rows(ref, member, row, value):
    flat, where = strided(ref, member, row)
    flat[where, :] = value


def collide(load, rate, store):
    weight = {shell: WEIGHTS[m] for m in range(Q) for shell in [SHELLS[square(m)]]}
    total = {}
    odd = {}
    for member in range(Q):
        vector = SPEEDS[member]
        shell = SHELLS[square(member)]
        opposite = INDEX[tuple(-value for value in vector)]
        if member == opposite:
            total[shell] = load(member)
        elif member < opposite:
            one, other = load(member), load(opposite)
            both = one + other
            total[shell] = total[shell] + both if shell in total else both
            odd[member] = one - other
    density = sum(weight[shell] * total[shell] for shell in total)
    energy = sum(weight[SHELLS[v]] * v * total[SHELLS[v]] for v in (1.0, 3.0, 4.0, 8.0, 9.0))
    inverse = 1.0 / density
    drift = []
    for axis in range(3):
        parts = {}
        for member, value in odd.items():
            speed = SPEEDS[member][axis]
            if speed == 0:
                continue
            key = (SHELLS[square(member)], abs(speed))
            if key in parts:
                parts[key] = parts[key] + value if speed > 0 else parts[key] - value
            else:
                parts[key] = value if speed > 0 else -value
        flux = sum((weight[shell] * speed * 1.5) * value for (shell, speed), value in parts.items())
        drift.append(flux * inverse)
    w = drift
    ww = [value * value for value in w]
    norm = (ww[0] + ww[1] + ww[2]) * (4.0 / 9.0)
    t = (energy * inverse - norm) * 0.5 - 1.0
    b = 1.5 * norm
    scale = rate * density
    keep = 1.0 - rate
    tb = t * b
    t2 = t * t
    p0 = scale * (1.0 - 0.5 * b + 0.125 * b * b - 1.5 * t + 1.25 * tb + 1.875 * t2)
    p1 = scale * (0.5 * t - 0.25 * tb - 1.25 * t2)
    p2 = scale * (0.125 * t2)
    st = scale * t
    b0 = scale * (0.5 - 0.25 * b) - 1.75 * st
    c0 = scale * (1.0 - 0.5 * b) - 2.5 * st
    quart = {k: (k**4 / 24.0) * scale for k in (1, 2, 3)}
    cubic = {k: (k**3 / 6.0) * scale for k in (1, 2, 3)}
    reach = {"1": 1, "c": 1, "2": 2, "e": 2, "3": 3}
    coefficients = {}
    for value, shell in SHELLS.items():
        s = 1.5 * value
        even = p0 + s * p1 + (s * s) * p2 if s else p0
        if s:
            k = reach[shell]
            coefficients[shell] = (
                even,
                (k * k) * b0 + (k * k * s * 0.25) * st,
                k * c0 + (k * s * 0.5) * st,
                quart[k],
                cubic[k],
            )
        else:
            coefficients[shell] = even
    for member in range(Q):
        vector = SPEEDS[member]
        shell = SHELLS[square(member)]
        opposite = INDEX[tuple(-value for value in vector)]
        if member == opposite:
            store(member, keep * load(member) + coefficients[shell])
        elif member < opposite:
            k = reach[shell]
            q, q2 = None, None
            axes = [axis for axis in range(3) if vector[axis] != 0]
            if len(axes) == 1:
                q, q2 = w[axes[0]], ww[axes[0]]
            else:
                q = w[axes[0]]
                for axis in axes[1:]:
                    q = q + w[axis] if vector[axis] > 0 else q - w[axis]
                q2 = q * q
            e0, e2, o1, e4, o3 = coefficients[shell]
            even = e0 + q2 * (e2 + q2 * e4)
            uneven = q * (o1 + q2 * o3)
            store(member, keep * load(member) + (even + uneven))
            store(opposite, keep * load(opposite) + (even - uneven))


def exchange_kernel(
    sizes, g_hbm, r_hbm, p_ref, up_ref, down_ref,
    g, rate, zraw, zsend, zrecv, ysend, yrecv, dsend, drecv,
    load_sem, z_sem, y_sem, d_sem, x_sem,
):
    nx, ny, nz = sizes
    pairs = nx // 2
    blocks = ny // 8
    order = [pairs - 1, 0] + [pair for pair in range(pairs - 2, 0, -1)]
    around = {}
    for axis in ("gx", "gy", "gz"):
        me, count = lax.axis_index(axis), lax.axis_size(axis)
        around[axis] = {1: lax.rem(me + 1, count), -1: lax.rem(me + count - 1, count)}

    loads = {}
    for turn, pair in enumerate(order):
        layers = pl.ds(2 * pair, 2)
        loads[pair] = [
            pltpu.make_async_copy(g_hbm.at[:, layers], g.at[:, layers], load_sem.at[turn]),
        ]
    rate_load = pltpu.make_async_copy(r_hbm, rate, load_sem.at[pairs])
    rate_load.start()
    for pair in order:
        for copy in loads[pair]:
            copy.start()

    barrier = pltpu.get_barrier_semaphore()
    friends = [{axis: around[axis][sign]} for axis in ("gx", "gy", "gz") for sign in (1, -1)]
    friends += [{"gx": around["gx"][sx], "gy": around["gy"][sy]} for sx, sy in CORNERS]
    for friend in friends:
        pl.semaphore_signal(barrier, inc=1, device_id=friend, device_id_type=MESH)

    lane = lax.broadcasted_iota(jnp.int32, (8, nz), 1)
    pack_masks = {offset: lane >= offset for offset in sorted(set(ZS[1].values())) if offset}

    def row_of(member, x, block):
        vector = SPEEDS[member]
        return pl.ds(final_row(member) + vector[1] + 8 * block, 8)

    def collide_block(x, block):
        packed = {1: None, -1: None}

        def load(member):
            return g[member, x, pl.ds(8 * block, 8), :]

        def store(member, value):
            cz = SPEEDS[member][2]
            if cz != 0:
                p_ref[member, x, row_of(member, x, block), :] = pltpu.roll(value, cz % nz, 1)
                sign = 1 if cz > 0 else -1
                place = ZS[sign][member]
                shift = (place + max(cz, 0)) % nz
                pieces.setdefault(sign, {})[place] = pltpu.roll(value, shift, 1) if shift else value
            else:
                p_ref[member, x, row_of(member, x, block), :] = value

        pieces = {}
        collide(load, rate[x, pl.ds(8 * block, 8), :], store)
        for index, sign in enumerate((1, -1)):
            packed = None
            for place in sorted(pieces[sign]):
                packed = pieces[sign][place] if packed is None else jnp.where(pack_masks[place], pieces[sign][place], packed)
            zraw[index, x, block] = packed

    def collide_pair(pair):
        def body(half, carry):
            for block in range(blocks):
                collide_block(2 * pair + half, block)
            return carry

        lax.fori_loop(0, 2, body, 0)

    def z_copy(pair, index):
        sign = (1, -1)[index]
        return pltpu.make_async_remote_copy(
            zsend.at[index, pair], zrecv.at[index, pair], z_sem.at[0, index, pair], z_sem.at[1, index, pair],
            device_id={"gz": around["gz"][sign]}, device_id_type=MESH,
        )

    def send_z(pair):
        for index in range(2):
            packed = None
            for half in range(2):
                for block in range(blocks):
                    place = 18 * (half * blocks + block)
                    value = zraw[index, 2 * pair + half, block]
                    packed = value if packed is None else jnp.where(lane >= place, pltpu.roll(value, place, 1), packed)
            zsend[index, pair] = packed
        for index in range(2):
            z_copy(pair, index).start()

    def merge_z(pair):
        for index, sign in enumerate((1, -1)):
            z_copy(pair, index).wait_recv()
            columns = zrecv[index, pair]
            for half in range(2):
                for block in range(blocks):
                    for member, offset in ZS[sign].items():
                        reach = abs(SPEEDS[member][2])
                        place = 18 * (half * blocks + block) + offset
                        target = 0 if sign > 0 else nz - reach
                        shift = (target - place) % nz
                        value = pltpu.roll(columns, shift, 1) if shift else columns
                        mask = lane < reach if sign > 0 else lane >= nz - reach
                        rows = row_of(member, 0, block)
                        pltpu.store(p_ref.at[member, 2 * pair + half, rows, :], value, mask=mask)

    halo = {1: up_ref, -1: down_ref}

    def x_copies(sign, members):
        copies = []
        for member in members:
            reach = abs(SPEEDS[member][0])
            rows = pl.ds(final_row(member), ny)
            layers = pl.ds(nx - reach, reach) if sign > 0 else pl.ds(0, reach)
            offset = XS[sign][member]
            place = list(XS[sign]).index(member)
            index = 0 if sign > 0 else 1
            copies.append(pltpu.make_async_remote_copy(
                p_ref.at[member, layers, rows, :], halo[sign].at[pl.ds(offset, reach), rows, :],
                x_sem.at[0, index, place], x_sem.at[1, index, place],
                device_id={"gx": around["gx"][sign]}, device_id_type=MESH,
            ))
        return copies

    def send_x(sign, members):
        for copy in x_copies(sign, members):
            copy.start()

    def d_copy(number):
        sx, sy = CORNERS[number]
        return pltpu.make_async_remote_copy(
            dsend.at[number], drecv.at[number], d_sem.at[0, number], d_sem.at[1, number],
            device_id={"gx": around["gx"][sx], "gy": around["gy"][sy]}, device_id_type=MESH,
        )

    def send_corners(sx):
        for number in range(4):
            if CORNERS[number][0] != sx:
                continue
            for place, (member, layer, row) in enumerate(corner_rows(*CORNERS[number])):
                x = nx - abs(SPEEDS[member][0]) + layer if sx > 0 else layer
                dsend[number, pl.ds(place, 1), :] = p_ref[member, x, pl.ds(leaving_row(member, row, ny), 1), :]
            d_copy(number).start()

    def y_copy(index):
        return pltpu.make_async_remote_copy(
            ysend.at[index], yrecv.at[index], y_sem.at[0, index], y_sem.at[1, index],
            device_id={"gy": around["gy"][(1, -1)[index]]}, device_id_type=MESH,
        )

    def send_y():
        for index, sign in enumerate((1, -1)):
            for member, offset in YS[sign].items():
                for row in range(abs(SPEEDS[member][1])):
                    ysend[index, offset + row] = read_rows(p_ref, member, leaving_row(member, row, ny))
            y_copy(index).start()

    def merge_y():
        for index, sign in enumerate((1, -1)):
            y_copy(index).wait_recv()
            for member, offset in YS[sign].items():
                for row in range(abs(SPEEDS[member][1])):
                    write_rows(p_ref, member, entering_row(member, row, ny), yrecv[index, offset + row])

    rate_load.wait()
    for turn, pair in enumerate(order):
        for copy in loads[pair]:
            copy.wait()
        collide_pair(pair)
        if turn == 0:
            pl.semaphore_wait(barrier, len(friends))
        send_z(pair)
        if turn == 0:
            send_x(1, EARLY[1])
        elif turn == 1:
            send_x(-1, EARLY[-1])
        elif pair == pairs - 2:
            send_x(1, THIRD[1])
        if pair == 1:
            send_x(-1, THIRD[-1])
    for turn, pair in enumerate(order):
        merge_z(pair)
        if turn < 2:
            sign = 1 if turn == 0 else -1
            send_x(sign, LATE[sign])
            send_corners(sign)
    send_y()
    for sign in (1, -1):
        for copy in x_copies(sign, list(XS[sign])):
            copy.wait_send()
    merge_y()
    for sign in (1, -1):
        for copy in x_copies(sign, list(XS[sign])):
            copy.wait_recv()
    for number, (sx, sy) in enumerate(CORNERS):
        d_copy(number).wait_recv()
        for place, (member, layer, row) in enumerate(corner_rows(sx, sy)):
            target = halo[sx]
            target[XS[sx][member] + layer, pl.ds(entering_row(member, row, ny), 1), :] = drecv[number, pl.ds(place, 1), :]
    for pair in order:
        for index in range(2):
            z_copy(pair, index).wait_send()
    for index in range(2):
        y_copy(index).wait_send()
    for number in range(4):
        d_copy(number).wait_send()


def emit_kernel(sizes, p_ref, up_ref, down_ref, o_hbm, sem):
    nx, ny, nz = sizes
    copies = []
    for member in range(Q):
        cx = SPEEDS[member][0]
        rows = pl.ds(final_row(member), ny)
        if cx > 0:
            pieces = [
                (p_ref.at[member, pl.ds(0, nx - cx), rows, :], o_hbm.at[member, pl.ds(cx, nx - cx)]),
                (up_ref.at[pl.ds(XS[1][member], cx), rows, :], o_hbm.at[member, pl.ds(0, cx)]),
            ]
        elif cx < 0:
            pieces = [
                (p_ref.at[member, pl.ds(-cx, nx + cx), rows, :], o_hbm.at[member, pl.ds(0, nx + cx)]),
                (down_ref.at[pl.ds(XS[-1][member], -cx), rows, :], o_hbm.at[member, pl.ds(nx + cx, -cx)]),
            ]
        else:
            pieces = [(p_ref.at[member, :, rows, :], o_hbm.at[member])]
        for source, target in pieces:
            copies.append(pltpu.make_async_copy(source, target, sem.at[len(copies)]))
    for copy in copies:
        copy.start()
    for copy in copies:
        copy.wait()


def per_device(populations, relax):
    sizes = populations.shape[1:]
    nx, ny, nz = sizes
    pairs, blocks = nx // 2, ny // 8
    vmem = pl.BlockSpec(memory_space=pltpu.VMEM)
    hbm = pl.BlockSpec(memory_space=pltpu.HBM)
    dma = pltpu.SemaphoreType.DMA
    shifted, up, down = pl.pallas_call(
        functools.partial(exchange_kernel, sizes),
        out_shape=(
            jax.ShapeDtypeStruct((Q, nx, ROWS, nz), F32),
            jax.ShapeDtypeStruct((18, ROWS, nz), F32),
            jax.ShapeDtypeStruct((18, ROWS, nz), F32),
        ),
        in_specs=[hbm, hbm],
        out_specs=(vmem, vmem, vmem),
        scratch_shapes=[
            pltpu.VMEM((Q, nx, ny, nz), F32),
            pltpu.VMEM((nx, ny, nz), F32),
            pltpu.VMEM((2, nx, blocks, 8, nz), F32),
            pltpu.VMEM((2, pairs, 8, nz), F32),
            pltpu.VMEM((2, pairs, 8, nz), F32),
            pltpu.VMEM((2, 18, nx, nz), F32),
            pltpu.VMEM((2, 18, nx, nz), F32),
            pltpu.VMEM((4, 8, nz), F32),
            pltpu.VMEM((4, 8, nz), F32),
            dma((pairs + 1,)),
            dma((2, 2, pairs)),
            dma((2, 2)),
            dma((2, 4)),
            dma((2, 2, 11)),
        ],
        compiler_params=pltpu.CompilerParams(
            collective_id=0, has_side_effects=True, vmem_limit_bytes=24 * 1024 * 1024
        ),
        name="collide_exchange",
    )(*(pltpu.with_memory_space_constraint(array, pltpu.HBM) for array in (populations, relax)))
    return pl.pallas_call(
        functools.partial(emit_kernel, sizes),
        out_shape=jax.ShapeDtypeStruct(populations.shape, F32),
        in_specs=[vmem, vmem, vmem],
        out_specs=hbm,
        scratch_shapes=[dma((61,))],
        compiler_params=pltpu.CompilerParams(vmem_limit_bytes=24 * 1024 * 1024),
        name="emit",
    )(shifted, up, down)


def solution(mesh):
    return jax.shard_map(
        per_device,
        mesh=mesh,
        in_specs=(P(None, "gx", "gy", "gz"), P("gx", "gy", "gz")),
        out_specs=P(None, "gx", "gy", "gz"),
        check_vma=False,
    )
```

time: 105 us -> 24.6 us (0.23)
  the two profiles are of different devices: /device:TPU:1 before, /device:TPU:9 now
where the time goes in v1:
time: 24.6 us
  Pallas kernels  24.6 us (100%)
    pallas_call x1, Pallas kernels, per_device(): pl.pallas_call(functools.partial(exchange_kernel, sizes), out_shape=(jax....  22.2 us
    pallas_call x1, Pallas kernels, per_device(): pl.pallas_call(functools.partial(emit_kernel, sizes), out_shape=jax.Shape...  2.4 us

profile of v1, /device:TPU:9, one launch (start us, length us, event | category | flops | bytes accessed | tf_op | source)
XLA Modules:
  0.0 24.6 jit_solution(10503636332461883733)
XLA Ops:
  0.0 22.2 %collide_exchange.1 = (f32[39,8,32,128]{3,2,1,0:T(8,128)S(1)}, f32[18,32,128]{2,1,0:T(8,128)S(1)}, f32[18,32,128]{2,1,0:T(8,128)S(1)}) custom-call(f32[39,8,24,128]{3,2,1,0:T(8,128)} %g_hbm.1, f32[8,24,128]{2,1,0:T(8,128)} %r_hbm.1), custom_call_target="tpu_custom_call" | custom-call | tf_op jit(solution)/shard_map/collide_exchange/pallas_call | solution.py:450
  22.2 2.4 %emit.1 = f32[39,8,24,128]{3,2,1,0:T(8,128)} custom-call(f32[39,8,32,128]{3,2,1,0:T(8,128)S(1)} %get-tuple-element.8.p_ref, f32[18,32,128]{2,1,0:T(8,128)S(1)} %get-tuple-element.9.up_ref, f32[18,32,128]{2,1,0:T(8,128)S(1)} %get-tuple-element.10.down_ref), custom_call_target="tpu_custom_call" | custom-call | tf_op jit(solution)/shard_map/emit/pallas_call | solution.py:480

commit v2 on v1

--- a/solution.py
+++ b/solution.py
@@ -56,20 +56,22 @@
 
 def slots(axis, sign):
     table, offset = {}, 0
-    for member in range(Q):
-        speed = SPEEDS[member][axis] * sign
-        if speed > 0:
-            table[member] = offset
-            offset += speed
+    for third in (0, 1, -1):
+        for member in range(Q):
+            speed = SPEEDS[member][axis] * sign
+            cz = SPEEDS[member][2] if axis < 2 else 0
+            if speed > 0 and (cz > 0) - (cz < 0) == third:
+                table[member] = offset
+                offset += speed
     return table
 
 
 XS = {sign: slots(0, sign) for sign in (1, -1)}
 YS = {sign: slots(1, sign) for sign in (1, -1)}
 ZS = {sign: slots(2, sign) for sign in (1, -1)}
-EARLY = {sign: [m for m in XS[sign] if SPEEDS[m][2] == 0 and abs(SPEEDS[m][0]) < 3] for sign in (1, -1)}
-THIRD = {sign: [m for m in XS[sign] if abs(SPEEDS[m][0]) == 3] for sign in (1, -1)}
-LATE = {sign: [m for m in XS[sign] if SPEEDS[m][2] != 0] for sign in (1, -1)}
+FLAT = {sign: [m for m in XS[sign] if SPEEDS[m][2] == 0] for sign in (1, -1)}
+TILTED = {sign: [m for m in XS[sign] if SPEEDS[m][2] != 0] for sign in (1, -1)}
+EDGE = 4
 CORNERS = [(1, 1), (1, -1), (-1, 1), (-1, -1)]
 SHELLS = {0.0: "0", 1.0: "1", 3.0: "c", 4.0: "2", 8.0: "e", 9.0: "3"}
 
@@ -207,45 +209,38 @@
 
 def exchange_kernel(
     sizes, g_hbm, r_hbm, p_ref, up_ref, down_ref,
-    g, rate, zraw, zsend, zrecv, ysend, yrecv, dsend, drecv,
-    load_sem, z_sem, y_sem, d_sem, x_sem,
+    g, rate, zraw, zsend, zrecv, xzrecv, ysend, yrecv, yzrecv, dsend, drecv, dzrecv,
+    load_sem, z_sem, xz_sem, y_sem, yz_sem, d_sem, dz_sem, x_sem, ready_sem, far_sem,
 ):
     nx, ny, nz = sizes
-    pairs = nx // 2
     blocks = ny // 8
-    order = [pairs - 1, 0] + [pair for pair in range(pairs - 2, 0, -1)]
+    signs = (1, -1)
     around = {}
     for axis in ("gx", "gy", "gz"):
         me, count = lax.axis_index(axis), lax.axis_size(axis)
         around[axis] = {1: lax.rem(me + 1, count), -1: lax.rem(me + count - 1, count)}
 
-    loads = {}
-    for turn, pair in enumerate(order):
-        layers = pl.ds(2 * pair, 2)
-        loads[pair] = [
-            pltpu.make_async_copy(g_hbm.at[:, layers], g.at[:, layers], load_sem.at[turn]),
-        ]
-    rate_load = pltpu.make_async_copy(r_hbm, rate, load_sem.at[pairs])
+    def layer_load(x):
+        return pltpu.make_async_copy(g_hbm.at[:, pl.ds(x, 1)], g.at[:, pl.ds(x, 1)], load_sem.at[x])
+
+    rate_load = pltpu.make_async_copy(r_hbm, rate, load_sem.at[nx])
     rate_load.start()
-    for pair in order:
-        for copy in loads[pair]:
-            copy.start()
+    for x in range(nx):
+        layer_load(x).start()
 
     barrier = pltpu.get_barrier_semaphore()
-    friends = [{axis: around[axis][sign]} for axis in ("gx", "gy", "gz") for sign in (1, -1)]
-    friends += [{"gx": around["gx"][sx], "gy": around["gy"][sy]} for sx, sy in CORNERS]
-    for friend in friends:
-        pl.semaphore_signal(barrier, inc=1, device_id=friend, device_id_type=MESH)
+    for axis in ("gx", "gy", "gz"):
+        for sign in signs:
+            pl.semaphore_signal(barrier, inc=1, device_id={axis: around[axis][sign]}, device_id_type=MESH)
 
     lane = lax.broadcasted_iota(jnp.int32, (8, nz), 1)
     pack_masks = {offset: lane >= offset for offset in sorted(set(ZS[1].values())) if offset}
 
-    def row_of(member, x, block):
-        vector = SPEEDS[member]
-        return pl.ds(final_row(member) + vector[1] + 8 * block, 8)
+    def row_of(member, block):
+        return pl.ds(final_row(member) + SPEEDS[member][1] + 8 * block, 8)
 
     def collide_block(x, block):
-        packed = {1: None, -1: None}
+        pieces = {1: {}, -1: {}}
 
         def load(member):
             return g[member, x, pl.ds(8 * block, 8), :]
@@ -253,165 +248,217 @@
         def store(member, value):
             cz = SPEEDS[member][2]
             if cz != 0:
-                p_ref[member, x, row_of(member, x, block), :] = pltpu.roll(value, cz % nz, 1)
+                p_ref[member, x, row_of(member, block), :] = pltpu.roll(value, cz % nz, 1)
                 sign = 1 if cz > 0 else -1
                 place = ZS[sign][member]
                 shift = (place + max(cz, 0)) % nz
-                pieces.setdefault(sign, {})[place] = pltpu.roll(value, shift, 1) if shift else value
+                pieces[sign][place] = pltpu.roll(value, shift, 1) if shift else value
             else:
-                p_ref[member, x, row_of(member, x, block), :] = value
-
-        pieces = {}
+                p_ref[member, x, row_of(member, block), :] = value
+
         collide(load, rate[x, pl.ds(8 * block, 8), :], store)
-        for index, sign in enumerate((1, -1)):
+        for index, sign in enumerate(signs):
             packed = None
             for place in sorted(pieces[sign]):
                 packed = pieces[sign][place] if packed is None else jnp.where(pack_masks[place], pieces[sign][place], packed)
             zraw[index, x, block] = packed
 
-    def collide_pair(pair):
-        def body(half, carry):
+    def collide_layer(x, carry):
+        layer_load(x).wait()
+        for block in range(blocks):
+            collide_block(x, block)
+        return carry
+
+    def column(half, block, offset):
+        return 18 * (half * blocks + block) + offset
+
+    def fold_z(index, pair):
+        packed = None
+        for half in range(2):
             for block in range(blocks):
-                collide_block(2 * pair + half, block)
-            return carry
-
-        lax.fori_loop(0, 2, body, 0)
-
-    def z_copy(pair, index):
-        sign = (1, -1)[index]
-        return pltpu.make_async_remote_copy(
-            zsend.at[index, pair], zrecv.at[index, pair], z_sem.at[0, index, pair], z_sem.at[1, index, pair],
-            device_id={"gz": around["gz"][sign]}, device_id_type=MESH,
-        )
-
-    def send_z(pair):
-        for index in range(2):
-            packed = None
-            for half in range(2):
-                for block in range(blocks):
-                    place = 18 * (half * blocks + block)
-                    value = zraw[index, 2 * pair + half, block]
-                    packed = value if packed is None else jnp.where(lane >= place, pltpu.roll(value, place, 1), packed)
-            zsend[index, pair] = packed
-        for index in range(2):
-            z_copy(pair, index).start()
-
-    def merge_z(pair):
-        for index, sign in enumerate((1, -1)):
-            z_copy(pair, index).wait_recv()
+                place = column(half, block, 0)
+                value = zraw[index, 2 * pair + half, block]
+                packed = value if packed is None else jnp.where(lane >= place, pltpu.roll(value, place, 1), packed)
+        zsend[index, pair] = packed
+
+    def enters(sign, reach):
+        return lane < reach if sign > 0 else lane >= nz - reach
+
+    def unfold(columns, target, member, half, block, rows):
+        cz = SPEEDS[member][2]
+        sign, reach = (1, cz) if cz > 0 else (-1, -cz)
+        place = column(half, block, ZS[sign][member])
+        shift = ((0 if sign > 0 else nz - reach) - place) % nz
+        value = pltpu.roll(columns, shift, 1) if shift else columns
+        pltpu.store(target.at[rows, :], value, mask=enters(sign, reach))
+
+    def z_copy(index):
+        return pltpu.make_async_remote_copy(
+            zsend.at[index], zrecv.at[index], z_sem.at[0, index], z_sem.at[1, index],
+            device_id={"gz": around["gz"][signs[index]]}, device_id_type=MESH,
+        )
+
+    def xz_copy(ix, iz):
+        pair = nx // 2 - 1 if ix == 0 else 0
+        return pltpu.make_async_remote_copy(
+            zsend.at[iz, pair], xzrecv.at[ix, iz], xz_sem.at[0, ix, iz], xz_sem.at[1, ix, iz],
+            device_id={"gx": around["gx"][signs[ix]], "gz": around["gz"][signs[iz]]}, device_id_type=MESH,
+        )
+
+    halo = (up_ref, down_ref)
+
+    def x_copy(ix, member):
+        sign, reach = signs[ix], abs(SPEEDS[member][0])
+        rows = pl.ds(final_row(member), ny)
+        layers = pl.ds(nx - reach, reach) if sign > 0 else pl.ds(0, reach)
+        place = list(XS[sign]).index(member)
+        return pltpu.make_async_remote_copy(
+            p_ref.at[member, layers, rows, :], halo[ix].at[pl.ds(XS[sign][member], reach), rows, :],
+            x_sem.at[0, ix, place], x_sem.at[1, ix, place],
+            device_id={"gx": around["gx"][sign]}, device_id_type=MESH,
+        )
+
+    def d_copy(number):
+        sx, sy = CORNERS[number]
+        return pltpu.make_async_remote_copy(
+            dsend.at[number], drecv.at[number], d_sem.at[0, number], d_sem.at[1, number],
+            device_id={"gx": around["gx"][sx], "gy": around["gy"][sy]}, device_id_type=MESH,
+        )
+
+    def dz_copy(number, iz):
+        sx, sy = CORNERS[number]
+        return pltpu.make_async_remote_copy(
+            dsend.at[number], dzrecv.at[number, iz], dz_sem.at[0, number, iz], dz_sem.at[1, number, iz],
+            device_id={"gx": around["gx"][sx], "gy": around["gy"][sy], "gz": around["gz"][signs[iz]]},
+            device_id_type=MESH,
+        )
+
+    def y_copy(iy):
+        return pltpu.make_async_remote_copy(
+            ysend.at[iy], yrecv.at[iy], y_sem.at[0, iy], y_sem.at[1, iy],
+            device_id={"gy": around["gy"][signs[iy]]}, device_id_type=MESH,
+        )
+
+    def yz_copy(iy, iz):
+        return pltpu.make_async_remote_copy(
+            ysend.at[iy, pl.ds(18 - (2 - iz) * EDGE, EDGE)], yzrecv.at[iy, iz],
+            yz_sem.at[0, iy, iz], yz_sem.at[1, iy, iz],
+            device_id={"gy": around["gy"][signs[iy]], "gz": around["gz"][signs[iz]]}, device_id_type=MESH,
+        )
+
+    rate_load.wait()
+    lax.fori_loop(0, nx, collide_layer, 0)
+    pl.semaphore_wait(barrier, 6)
+    for axis in ("gy", "gz"):
+        for sign in signs:
+            pl.semaphore_signal(ready_sem, inc=1, device_id={axis: around[axis][sign]}, device_id_type=MESH)
+    for members in (TILTED, FLAT):
+        for ix, sign in enumerate(signs):
+            for member in members[sign]:
+                x_copy(ix, member).start()
+    for index in range(2):
+        for pair in range(nx // 2):
+            fold_z(index, pair)
+    for index in range(2):
+        z_copy(index).start()
+    for iy, sign in enumerate(signs):
+        for member, offset in YS[sign].items():
+            for row in range(abs(SPEEDS[member][1])):
+                ysend[iy, offset + row] = read_rows(p_ref, member, leaving_row(member, row, ny))
+        y_copy(iy).start()
+    for number, (sx, sy) in enumerate(CORNERS):
+        for place, (member, layer, row) in enumerate(corner_rows(sx, sy)):
+            x = nx - abs(SPEEDS[member][0]) + layer if sx > 0 else layer
+            dsend[number, pl.ds(place, 1), :] = p_ref[member, x, pl.ds(leaving_row(member, row, ny), 1), :]
+    pl.semaphore_wait(ready_sem, 4)
+    for sign in signs:
+        pl.semaphore_signal(far_sem, inc=1, device_id={"gz": around["gz"][sign]}, device_id_type=MESH)
+    for number in range(4):
+        d_copy(number).start()
+    for ix in range(2):
+        for iz in range(2):
+            xz_copy(ix, iz).start()
+    for iy in range(2):
+        for iz in range(2):
+            yz_copy(iy, iz).start()
+    pl.semaphore_wait(far_sem, 2)
+    for number in range(4):
+        for iz in range(2):
+            dz_copy(number, iz).start()
+
+    def merge_z(index, wanted):
+        for pair in range(nx // 2):
             columns = zrecv[index, pair]
             for half in range(2):
                 for block in range(blocks):
-                    for member, offset in ZS[sign].items():
-                        reach = abs(SPEEDS[member][2])
-                        place = 18 * (half * blocks + block) + offset
-                        target = 0 if sign > 0 else nz - reach
-                        shift = (target - place) % nz
-                        value = pltpu.roll(columns, shift, 1) if shift else columns
-                        mask = lane < reach if sign > 0 else lane >= nz - reach
-                        rows = row_of(member, 0, block)
-                        pltpu.store(p_ref.at[member, 2 * pair + half, rows, :], value, mask=mask)
-
-    halo = {1: up_ref, -1: down_ref}
-
-    def x_copies(sign, members):
-        copies = []
-        for member in members:
-            reach = abs(SPEEDS[member][0])
-            rows = pl.ds(final_row(member), ny)
-            layers = pl.ds(nx - reach, reach) if sign > 0 else pl.ds(0, reach)
-            offset = XS[sign][member]
-            place = list(XS[sign]).index(member)
-            index = 0 if sign > 0 else 1
-            copies.append(pltpu.make_async_remote_copy(
-                p_ref.at[member, layers, rows, :], halo[sign].at[pl.ds(offset, reach), rows, :],
-                x_sem.at[0, index, place], x_sem.at[1, index, place],
-                device_id={"gx": around["gx"][sign]}, device_id_type=MESH,
-            ))
-        return copies
-
-    def send_x(sign, members):
-        for copy in x_copies(sign, members):
-            copy.start()
-
-    def d_copy(number):
-        sx, sy = CORNERS[number]
-        return pltpu.make_async_remote_copy(
-            dsend.at[number], drecv.at[number], d_sem.at[0, number], d_sem.at[1, number],
-            device_id={"gx": around["gx"][sx], "gy": around["gy"][sy]}, device_id_type=MESH,
-        )
-
-    def send_corners(sx):
-        for number in range(4):
-            if CORNERS[number][0] != sx:
-                continue
-            for place, (member, layer, row) in enumerate(corner_rows(*CORNERS[number])):
-                x = nx - abs(SPEEDS[member][0]) + layer if sx > 0 else layer
-                dsend[number, pl.ds(place, 1), :] = p_ref[member, x, pl.ds(leaving_row(member, row, ny), 1), :]
-            d_copy(number).start()
-
-    def y_copy(index):
-        return pltpu.make_async_remote_copy(
-            ysend.at[index], yrecv.at[index], y_sem.at[0, index], y_sem.at[1, index],
-            device_id={"gy": around["gy"][(1, -1)[index]]}, device_id_type=MESH,
-        )
-
-    def send_y():
-        for index, sign in enumerate((1, -1)):
-            for member, offset in YS[sign].items():
-                for row in range(abs(SPEEDS[member][1])):
-                    ysend[index, offset + row] = read_rows(p_ref, member, leaving_row(member, row, ny))
-            y_copy(index).start()
-
-    def merge_y():
-        for index, sign in enumerate((1, -1)):
-            y_copy(index).wait_recv()
-            for member, offset in YS[sign].items():
-                for row in range(abs(SPEEDS[member][1])):
-                    write_rows(p_ref, member, entering_row(member, row, ny), yrecv[index, offset + row])
-
-    rate_load.wait()
-    for turn, pair in enumerate(order):
-        for copy in loads[pair]:
-            copy.wait()
-        collide_pair(pair)
-        if turn == 0:
-            pl.semaphore_wait(barrier, len(friends))
-        send_z(pair)
-        if turn == 0:
-            send_x(1, EARLY[1])
-        elif turn == 1:
-            send_x(-1, EARLY[-1])
-        elif pair == pairs - 2:
-            send_x(1, THIRD[1])
-        if pair == 1:
-            send_x(-1, THIRD[-1])
-    for turn, pair in enumerate(order):
-        merge_z(pair)
-        if turn < 2:
-            sign = 1 if turn == 0 else -1
-            send_x(sign, LATE[sign])
-            send_corners(sign)
-    send_y()
-    for sign in (1, -1):
-        for copy in x_copies(sign, list(XS[sign])):
-            copy.wait_send()
-    merge_y()
-    for sign in (1, -1):
-        for copy in x_copies(sign, list(XS[sign])):
-            copy.wait_recv()
+                    for member in ZS[signs[index]]:
+                        x = 2 * pair + half
+                        if wanted(member, x):
+                            unfold(columns, p_ref.at[member, x], member, half, block, row_of(member, block))
+
+    def travels(member, x):
+        cx = SPEEDS[member][0]
+        return x >= nx - cx if cx > 0 else x < -cx
+
+    for index in range(2):
+        z_copy(index).wait_recv()
+        merge_z(index, lambda member, x: not travels(member, x))
+    for members in (TILTED, FLAT):
+        for ix, sign in enumerate(signs):
+            for member in members[sign]:
+                x_copy(ix, member).wait_send()
+    for index in range(2):
+        merge_z(index, travels)
+    for iy, sign in enumerate(signs):
+        y_copy(iy).wait_recv()
+        for iz in range(2):
+            yz_copy(iy, iz).wait_recv()
+        for member, offset in YS[sign].items():
+            cz = SPEEDS[member][2]
+            for row in range(abs(SPEEDS[member][1])):
+                value = yrecv[iy, offset + row]
+                if cz != 0:
+                    iz = 0 if cz > 0 else 1
+                    edge = yzrecv[iy, iz, offset + row - 18 + (2 - iz) * EDGE]
+                    value = jnp.where(enters(signs[iz], abs(cz)), edge, value)
+                write_rows(p_ref, member, entering_row(member, row, ny), value)
+    for ix, sign in enumerate(signs):
+        for iz in range(2):
+            xz_copy(ix, iz).wait_recv()
+        for member in TILTED[sign]:
+            x_copy(ix, member).wait_recv()
+            reach, iz = abs(SPEEDS[member][0]), 0 if SPEEDS[member][2] > 0 else 1
+            for layer in range(reach):
+                half = 2 - reach + layer if sign > 0 else layer
+                for block in range(blocks):
+                    target = halo[ix].at[XS[sign][member] + layer]
+                    unfold(xzrecv[ix, iz], target, member, half, block, row_of(member, block))
+    for ix, sign in enumerate(signs):
+        for member in FLAT[sign]:
+            x_copy(ix, member).wait_recv()
     for number, (sx, sy) in enumerate(CORNERS):
+        ix = 0 if sx > 0 else 1
         d_copy(number).wait_recv()
+        for iz in range(2):
+            dz_copy(number, iz).wait_recv()
         for place, (member, layer, row) in enumerate(corner_rows(sx, sy)):
-            target = halo[sx]
-            target[XS[sx][member] + layer, pl.ds(entering_row(member, row, ny), 1), :] = drecv[number, pl.ds(place, 1), :]
-    for pair in order:
-        for index in range(2):
-            z_copy(pair, index).wait_send()
+            cz = SPEEDS[member][2]
+            value = drecv[number, pl.ds(place, 1), :]
+            if cz != 0:
+                iz = 0 if cz > 0 else 1
+                mask = enters(signs[iz], abs(cz))[:1]
+                value = jnp.where(mask, dzrecv[number, iz, pl.ds(place, 1), :], value)
+            halo[ix][XS[sx][member] + layer, pl.ds(entering_row(member, row, ny), 1), :] = value
     for index in range(2):
+        z_copy(index).wait_send()
         y_copy(index).wait_send()
+        for iz in range(2):
+            xz_copy(index, iz).wait_send()
+            yz_copy(index, iz).wait_send()
     for number in range(4):
         d_copy(number).wait_send()
+        for iz in range(2):
+            dz_copy(number, iz).wait_send()
 
 
 def emit_kernel(sizes, p_ref, up_ref, down_ref, o_hbm, sem):
@@ -443,7 +490,7 @@
 def per_device(populations, relax):
     sizes = populations.shape[1:]
     nx, ny, nz = sizes
-    pairs, blocks = nx // 2, ny // 8
+    blocks = ny // 8
     vmem = pl.BlockSpec(memory_space=pltpu.VMEM)
     hbm = pl.BlockSpec(memory_space=pltpu.HBM)
     dma = pltpu.SemaphoreType.DMA
@@ -460,17 +507,25 @@
             pltpu.VMEM((Q, nx, ny, nz), F32),
             pltpu.VMEM((nx, ny, nz), F32),
             pltpu.VMEM((2, nx, blocks, 8, nz), F32),
-            pltpu.VMEM((2, pairs, 8, nz), F32),
-            pltpu.VMEM((2, pairs, 8, nz), F32),
+            pltpu.VMEM((2, nx // 2, 8, nz), F32),
+            pltpu.VMEM((2, nx // 2, 8, nz), F32),
+            pltpu.VMEM((2, 2, 8, nz), F32),
             pltpu.VMEM((2, 18, nx, nz), F32),
             pltpu.VMEM((2, 18, nx, nz), F32),
+            pltpu.VMEM((2, 2, EDGE, nx, nz), F32),
             pltpu.VMEM((4, 8, nz), F32),
             pltpu.VMEM((4, 8, nz), F32),
-            dma((pairs + 1,)),
-            dma((2, 2, pairs)),
+            pltpu.VMEM((4, 2, 8, nz), F32),
+            dma((nx + 1,)),
             dma((2, 2)),
+            dma((2, 2, 2)),
+            dma((2, 2)),
+            dma((2, 2, 2)),
             dma((2, 4)),
+            dma((2, 4, 2)),
             dma((2, 2, 11)),
+            pltpu.SemaphoreType.REGULAR,
+            pltpu.SemaphoreType.REGULAR,
         ],
         compiler_params=pltpu.CompilerParams(
             collective_id=0, has_side_effects=True, vmem_limit_bytes=24 * 1024 * 1024

time: 24.6 us -> 22.7 us (0.923)
  the two profiles are of different devices: /device:TPU:9 before, /device:TPU:1 now
where the time goes in v2:
time: 22.7 us; the launch traced here: 22.6 us
  Pallas kernels  22.6 us (100%)
    pallas_call x1, Pallas kernels, per_device(): pl.pallas_call(functools.partial(exchange_kernel, sizes), out_shape=(jax....  20.2 us
    pallas_call x1, Pallas kernels, per_device(): pl.pallas_call(functools.partial(emit_kernel, sizes), out_shape=jax.Shape...  2.4 us

profile of v2, /device:TPU:1, one launch (start us, length us, event | category | flops | bytes accessed | tf_op | source)
XLA Modules:
  0.0 22.6 jit_solution(12041304513470946892)
XLA Ops:
  0.0 20.2 %collide_exchange.1 = (f32[39,8,32,128]{3,2,1,0:T(8,128)S(1)}, f32[18,32,128]{2,1,0:T(8,128)S(1)}, f32[18,32,128]{2,1,0:T(8,128)S(1)}) custom-call(f32[39,8,24,128]{3,2,1,0:T(8,128)} %g_hbm.1, f32[8,24,128]{2,1,0:T(8,128)} %r_hbm.1), custom_call_target="tpu_custom_call" | custom-call | tf_op jit(solution)/shard_map/collide_exchange/pallas_call | solution.py:497
  20.2 2.4 %emit.1 = f32[39,8,24,128]{3,2,1,0:T(8,128)} custom-call(f32[39,8,32,128]{3,2,1,0:T(8,128)S(1)} %get-tuple-element.8.p_ref, f32[18,32,128]{2,1,0:T(8,128)S(1)} %get-tuple-element.9.up_ref, f32[18,32,128]{2,1,0:T(8,128)S(1)} %get-tuple-element.10.down_ref), custom_call_target="tpu_custom_call" | custom-call | tf_op jit(solution)/shard_map/emit/pallas_call | solution.py:535

commit v3 on v2

--- a/solution.py
+++ b/solution.py
@@ -210,7 +210,7 @@
 def exchange_kernel(
     sizes, g_hbm, r_hbm, p_ref, up_ref, down_ref,
     g, rate, zraw, zsend, zrecv, xzrecv, ysend, yrecv, yzrecv, dsend, drecv, dzrecv,
-    load_sem, z_sem, xz_sem, y_sem, yz_sem, d_sem, dz_sem, x_sem, ready_sem, far_sem,
+    load_sem, z_sem, xz_sem, y_sem, yz_sem, d_sem, dz_sem, x_sem, pair_sem, plane_sem, ready_sem,
 ):
     nx, ny, nz = sizes
     blocks = ny // 8
@@ -225,13 +225,25 @@
 
     rate_load = pltpu.make_async_copy(r_hbm, rate, load_sem.at[nx])
     rate_load.start()
-    for x in range(nx):
+    for x in [nx - 1, nx - 2, 0, 1] + list(range(2, nx - 2)):
         layer_load(x).start()
 
     barrier = pltpu.get_barrier_semaphore()
-    for axis in ("gx", "gy", "gz"):
-        for sign in signs:
-            pl.semaphore_signal(barrier, inc=1, device_id={axis: around[axis][sign]}, device_id_type=MESH)
+    gz = lax.axis_index("gz")
+    core = lax.rem(gz, 2)
+    chip = gz - core
+    other_chip = lax.rem(chip + 2, lax.axis_size("gz"))
+    partner = chip + 1 - core
+
+    def tell(semaphore, **device):
+        pl.semaphore_signal(semaphore, inc=1, device_id=device, device_id_type=MESH)
+
+    for sign in signs:
+        tell(barrier, gx=around["gx"][sign], gz=chip)
+        tell(barrier, gy=around["gy"][sign], gz=chip + 1)
+    tell(barrier, gz=other_chip)
+
+    tell(barrier, gz=partner)
 
     lane = lax.broadcasted_iota(jnp.int32, (8, nz), 1)
     pack_masks = {offset: lane >= offset for offset in sorted(set(ZS[1].values())) if offset}
@@ -346,45 +358,114 @@
             device_id={"gy": around["gy"][signs[iy]], "gz": around["gz"][signs[iz]]}, device_id_type=MESH,
         )
 
+    def slabs(fast):
+        for members in (TILTED, FLAT):
+            for ix, sign in enumerate(signs):
+                for member in members[sign]:
+                    if (abs(SPEEDS[member][0]) == 3) == fast:
+                        x_copy(ix, member).start()
+
+    def meet(own, count):
+        @pl.when(core == own)
+        def _():
+            pl.semaphore_wait(barrier, count)
+            tell(pair_sem, gz=partner)
+
+        @pl.when(core != own)
+        def _():
+            pl.semaphore_wait(pair_sem, 1)
+
+    def meet_x():
+        meet(0, 7)
+
+    def meet_y():
+        meet(1, 5)
+
+    def corners(iy):
+        pl.semaphore_wait(ready_sem.at[iy], 1)
+        for number, (sx, sy) in enumerate(CORNERS):
+            if sy == signs[iy]:
+                d_copy(number).start()
+                for iz in range(2):
+                    dz_copy(number, iz).start()
+
+    def edges(iy):
+        for iz in range(2):
+            yz_copy(iy, iz).start()
+
+    last = lax.axis_index("gy") == lax.axis_size("gy") - 1
+    not_last = jnp.logical_not(last)
+    x_first = jnp.logical_and(not_last, lax.axis_index("gx") > 0)
     rate_load.wait()
-    lax.fori_loop(0, nx, collide_layer, 0)
-    pl.semaphore_wait(barrier, 6)
-    for axis in ("gy", "gz"):
-        for sign in signs:
-            pl.semaphore_signal(ready_sem, inc=1, device_id={axis: around[axis][sign]}, device_id_type=MESH)
-    for members in (TILTED, FLAT):
-        for ix, sign in enumerate(signs):
-            for member in members[sign]:
-                x_copy(ix, member).start()
+    lax.fori_loop(0, 2, lambda turn, carry: collide_layer(nx - 1 - turn, carry), 0)
+    lax.fori_loop(0, 2, collide_layer, 0)
+    for number, (sx, sy) in enumerate(CORNERS):
+        for place, (member, layer, row) in enumerate(corner_rows(sx, sy)):
+            x = nx - abs(SPEEDS[member][0]) + layer if sx > 0 else layer
+            dsend[number, pl.ds(place, 1), :] = p_ref[member, x, pl.ds(leaving_row(member, row, ny), 1), :]
+
+    @pl.when(x_first)
+    def _():
+        meet_x()
+        slabs(False)
+
+    @pl.when(last)
+    def _():
+        meet_y()
+        corners(0)
+
+    lax.fori_loop(2, nx - 2, collide_layer, 0)
+
+    @pl.when(x_first)
+    def _():
+        slabs(True)
+
+    for iy, sign in enumerate(signs):
+        for member, offset in YS[sign].items():
+            for row in range(abs(SPEEDS[member][1])):
+                ysend[iy, offset + row] = read_rows(p_ref, member, leaving_row(member, row, ny))
+
+    @pl.when(not_last)
+    def _():
+        meet_y()
+
+    for iy in range(2):
+        y_copy(iy).start()
+
+    @pl.when(last)
+    def _():
+        edges(0)
+
+    @pl.when(jnp.logical_not(x_first))
+    def _():
+        meet_x()
+
+    for sign in signs:
+        tell(plane_sem, gz=around["gz"][sign])
     for index in range(2):
         for pair in range(nx // 2):
             fold_z(index, pair)
     for index in range(2):
         z_copy(index).start()
+    pl.semaphore_wait(plane_sem, 2)
     for iy, sign in enumerate(signs):
-        for member, offset in YS[sign].items():
-            for row in range(abs(SPEEDS[member][1])):
-                ysend[iy, offset + row] = read_rows(p_ref, member, leaving_row(member, row, ny))
-        y_copy(iy).start()
-    for number, (sx, sy) in enumerate(CORNERS):
-        for place, (member, layer, row) in enumerate(corner_rows(sx, sy)):
-            x = nx - abs(SPEEDS[member][0]) + layer if sx > 0 else layer
-            dsend[number, pl.ds(place, 1), :] = p_ref[member, x, pl.ds(leaving_row(member, row, ny), 1), :]
-    pl.semaphore_wait(ready_sem, 4)
-    for sign in signs:
-        pl.semaphore_signal(far_sem, inc=1, device_id={"gz": around["gz"][sign]}, device_id_type=MESH)
-    for number in range(4):
-        d_copy(number).start()
+        tell(ready_sem.at[1 - iy], gy=around["gy"][sign])
     for ix in range(2):
         for iz in range(2):
             xz_copy(ix, iz).start()
-    for iy in range(2):
-        for iz in range(2):
-            yz_copy(iy, iz).start()
-    pl.semaphore_wait(far_sem, 2)
-    for number in range(4):
-        for iz in range(2):
-            dz_copy(number, iz).start()
+
+    @pl.when(jnp.logical_not(x_first))
+    def _():
+        slabs(False)
+        slabs(True)
+
+    @pl.when(not_last)
+    def _():
+        corners(0)
+        edges(0)
+
+    corners(1)
+    edges(1)
 
     def merge_z(index, wanted):
         for pair in range(nx // 2):
@@ -526,6 +607,7 @@
             dma((2, 2, 11)),
             pltpu.SemaphoreType.REGULAR,
             pltpu.SemaphoreType.REGULAR,
+            pltpu.SemaphoreType.REGULAR((2,)),
         ],
         compiler_params=pltpu.CompilerParams(
             collective_id=0, has_side_effects=True, vmem_limit_bytes=24 * 1024 * 1024

time: 22.7 us -> 22.3 us (0.982)
  the two profiles are of different devices: /device:TPU:1 before, /device:TPU:224 now
where the time goes in v3:
time: 22.3 us; the launch traced here: 22.2 us
  Pallas kernels  22.2 us (100%)
    pallas_call x1, Pallas kernels, per_device(): pl.pallas_call(functools.partial(exchange_kernel, sizes), out_shape=(jax....  19.8 us
    pallas_call x1, Pallas kernels, per_device(): pl.pallas_call(functools.partial(emit_kernel, sizes), out_shape=jax.Shape...  2.4 us

profile of v3, /device:TPU:224, one launch (start us, length us, event | category | flops | bytes accessed | tf_op | source)
XLA Modules:
  0.0 22.2 jit_solution(5441949610722694928)
XLA Ops:
  0.0 19.8 %collide_exchange.1 = (f32[39,8,32,128]{3,2,1,0:T(8,128)S(1)}, f32[18,32,128]{2,1,0:T(8,128)S(1)}, f32[18,32,128]{2,1,0:T(8,128)S(1)}) custom-call(f32[39,8,24,128]{3,2,1,0:T(8,128)} %g_hbm.1, f32[8,24,128]{2,1,0:T(8,128)} %r_hbm.1), custom_call_target="tpu_custom_call" | custom-call | tf_op jit(solution)/shard_map/collide_exchange/pallas_call | solution.py:578
  19.8 2.4 %emit.1 = f32[39,8,24,128]{3,2,1,0:T(8,128)} custom-call(f32[39,8,32,128]{3,2,1,0:T(8,128)S(1)} %get-tuple-element.8.p_ref, f32[18,32,128]{2,1,0:T(8,128)S(1)} %get-tuple-element.9.up_ref, f32[18,32,128]{2,1,0:T(8,128)S(1)} %get-tuple-element.10.down_ref), custom_call_target="tpu_custom_call" | custom-call | tf_op jit(solution)/shard_map/emit/pallas_call | solution.py:617

commit v4 on v3

--- a/solution.py
+++ b/solution.py
@@ -395,7 +395,8 @@
 
     last = lax.axis_index("gy") == lax.axis_size("gy") - 1
     not_last = jnp.logical_not(last)
-    x_first = jnp.logical_and(not_last, lax.axis_index("gx") > 0)
+    first = lax.axis_index("gy") == 0
+    x_first = lax.axis_index("gx") > 0
     rate_load.wait()
     lax.fori_loop(0, 2, lambda turn, carry: collide_layer(nx - 1 - turn, carry), 0)
     lax.fori_loop(0, 2, collide_layer, 0)
@@ -404,15 +405,15 @@
             x = nx - abs(SPEEDS[member][0]) + layer if sx > 0 else layer
             dsend[number, pl.ds(place, 1), :] = p_ref[member, x, pl.ds(leaving_row(member, row, ny), 1), :]
 
+    @pl.when(last)
+    def _():
+        meet_y()
+        corners(0)
+
     @pl.when(x_first)
     def _():
         meet_x()
         slabs(False)
-
-    @pl.when(last)
-    def _():
-        meet_y()
-        corners(0)
 
     lax.fori_loop(2, nx - 2, collide_layer, 0)
 
@@ -464,8 +465,11 @@
         corners(0)
         edges(0)
 
-    corners(1)
-    edges(1)
+    def finish_edges():
+        corners(1)
+        edges(1)
+
+    pl.when(jnp.logical_not(first))(finish_edges)
 
     def merge_z(index, wanted):
         for pair in range(nx // 2):
@@ -484,6 +488,7 @@
     for index in range(2):
         z_copy(index).wait_recv()
         merge_z(index, lambda member, x: not travels(member, x))
+    pl.when(first)(finish_edges)
     for members in (TILTED, FLAT):
         for ix, sign in enumerate(signs):
             for member in members[sign]:

time: 22.3 us -> 21.5 us (0.964)
  the two profiles are of different devices: /device:TPU:224 before, /device:TPU:225 now
where the time goes in v4:
time: 21.5 us; the launch traced here: 21.4 us
  Pallas kernels  21.4 us (100%)
    pallas_call x1, Pallas kernels, per_device(): pl.pallas_call(functools.partial(exchange_kernel, sizes), out_shape=(jax....  19 us
    pallas_call x1, Pallas kernels, per_device(): pl.pallas_call(functools.partial(emit_kernel, sizes), out_shape=jax.Shape...  2.4 us

profile of v4, /device:TPU:225, one launch (start us, length us, event | category | flops | bytes accessed | tf_op | source)
XLA Modules:
  0.0 21.4 jit_solution(4879084975465708088)
XLA Ops:
  0.0 19.0 %collide_exchange.1 = (f32[39,8,32,128]{3,2,1,0:T(8,128)S(1)}, f32[18,32,128]{2,1,0:T(8,128)S(1)}, f32[18,32,128]{2,1,0:T(8,128)S(1)}) custom-call(f32[39,8,24,128]{3,2,1,0:T(8,128)} %g_hbm.1, f32[8,24,128]{2,1,0:T(8,128)} %r_hbm.1), custom_call_target="tpu_custom_call" | custom-call | tf_op jit(solution)/shard_map/collide_exchange/pallas_call | solution.py:583
  19.0 2.4 %emit.1 = f32[39,8,24,128]{3,2,1,0:T(8,128)} custom-call(f32[39,8,32,128]{3,2,1,0:T(8,128)S(1)} %get-tuple-element.8.p_ref, f32[18,32,128]{2,1,0:T(8,128)S(1)} %get-tuple-element.9.up_ref, f32[18,32,128]{2,1,0:T(8,128)S(1)} %get-tuple-element.10.down_ref), custom_call_target="tpu_custom_call" | custom-call | tf_op jit(solution)/shard_map/emit/pallas_call | solution.py:622

commit v5 on v4

--- a/solution.py
+++ b/solution.py
@@ -405,16 +405,32 @@
             x = nx - abs(SPEEDS[member][0]) + layer if sx > 0 else layer
             dsend[number, pl.ds(place, 1), :] = p_ref[member, x, pl.ds(leaving_row(member, row, ny), 1), :]
 
+    def tell_plane():
+        for sign in signs:
+            tell(plane_sem, gz=around["gz"][sign])
+
+    def tell_ready():
+        pl.semaphore_wait(plane_sem, 2)
+        for iy, sign in enumerate(signs):
+            tell(ready_sem.at[1 - iy], gy=around["gy"][sign])
+
+    x_last = jnp.logical_not(x_first)
+    pl.when(last)(meet_y)
+
+    @pl.when(x_first)
+    def _():
+        meet_x()
+        tell_plane()
+
     @pl.when(last)
     def _():
-        meet_y()
         corners(0)
 
     @pl.when(x_first)
     def _():
-        meet_x()
         slabs(False)
 
+    pl.when(jnp.logical_and(last, x_first))(tell_ready)
     lax.fori_loop(2, nx - 2, collide_layer, 0)
 
     @pl.when(x_first)
@@ -426,10 +442,8 @@
             for row in range(abs(SPEEDS[member][1])):
                 ysend[iy, offset + row] = read_rows(p_ref, member, leaving_row(member, row, ny))
 
-    @pl.when(not_last)
-    def _():
-        meet_y()
-
+    pl.when(not_last)(meet_y)
+    pl.when(jnp.logical_and(not_last, x_first))(tell_ready)
     for iy in range(2):
         y_copy(iy).start()
 
@@ -437,20 +451,17 @@
     def _():
         edges(0)
 
-    @pl.when(jnp.logical_not(x_first))
+    @pl.when(x_last)
     def _():
         meet_x()
-
-    for sign in signs:
-        tell(plane_sem, gz=around["gz"][sign])
+        tell_plane()
+
     for index in range(2):
         for pair in range(nx // 2):
             fold_z(index, pair)
     for index in range(2):
         z_copy(index).start()
-    pl.semaphore_wait(plane_sem, 2)
-    for iy, sign in enumerate(signs):
-        tell(ready_sem.at[1 - iy], gy=around["gy"][sign])
+    pl.when(x_last)(tell_ready)
     for ix in range(2):
         for iz in range(2):
             xz_copy(ix, iz).start()

time: 21.5 us -> 20.7 us (0.963)
  the two profiles are of different devices: /device:TPU:225 before, /device:TPU:1 now
where the time goes in v5:
time: 20.7 us; the launch traced here: 20.6 us
  Pallas kernels  20.6 us (100%)
    pallas_call x1, Pallas kernels, per_device(): pl.pallas_call(functools.partial(exchange_kernel, sizes), out_shape=(jax....  18.2 us
    pallas_call x1, Pallas kernels, per_device(): pl.pallas_call(functools.partial(emit_kernel, sizes), out_shape=jax.Shape...  2.4 us

profile of v5, /device:TPU:1, one launch (start us, length us, event | category | flops | bytes accessed | tf_op | source)
XLA Modules:
  0.0 20.6 jit_solution(15300336862938508438)
XLA Ops:
  0.0 18.2 %collide_exchange.1 = (f32[39,8,32,128]{3,2,1,0:T(8,128)S(1)}, f32[18,32,128]{2,1,0:T(8,128)S(1)}, f32[18,32,128]{2,1,0:T(8,128)S(1)}) custom-call(f32[39,8,24,128]{3,2,1,0:T(8,128)} %g_hbm.1, f32[8,24,128]{2,1,0:T(8,128)} %r_hbm.1), custom_call_target="tpu_custom_call" | custom-call | tf_op jit(solution)/shard_map/collide_exchange/pallas_call | solution.py:594
  18.2 2.4 %emit.1 = f32[39,8,24,128]{3,2,1,0:T(8,128)} custom-call(f32[39,8,32,128]{3,2,1,0:T(8,128)S(1)} %get-tuple-element.8.p_ref, f32[18,32,128]{2,1,0:T(8,128)S(1)} %get-tuple-element.9.up_ref, f32[18,32,128]{2,1,0:T(8,128)S(1)} %get-tuple-element.10.down_ref), custom_call_target="tpu_custom_call" | custom-call | tf_op jit(solution)/shard_map/emit/pallas_call | solution.py:633

commit v6 on v5

--- a/solution.py
+++ b/solution.py
@@ -323,11 +323,23 @@
         sign, reach = signs[ix], abs(SPEEDS[member][0])
         rows = pl.ds(final_row(member), ny)
         layers = pl.ds(nx - reach, reach) if sign > 0 else pl.ds(0, reach)
-        place = list(XS[sign]).index(member)
+        place = group_of(member)
         return pltpu.make_async_remote_copy(
             p_ref.at[member, layers, rows, :], halo[ix].at[pl.ds(XS[sign][member], reach), rows, :],
             x_sem.at[0, ix, place], x_sem.at[1, ix, place],
             device_id={"gx": around["gx"][sign]}, device_id_type=MESH,
+        )
+
+    def group_of(member):
+        return 0 if SPEEDS[member][2] != 0 else 1 if abs(SPEEDS[member][0]) < 3 else 2
+
+    def x_group(ix, group):
+        members = [m for m in XS[signs[ix]] if group_of(m) == group]
+        count = sum(abs(SPEEDS[m][0]) for m in members)
+        layers = halo[ix].at[pl.ds(XS[signs[ix]][members[0]], count), pl.ds(0, ny), :]
+        return pltpu.make_async_remote_copy(
+            layers, layers, x_sem.at[0, ix, group], x_sem.at[1, ix, group],
+            device_id={"gx": around["gx"][signs[ix]]}, device_id_type=MESH,
         )
 
     def d_copy(number):
@@ -442,6 +454,15 @@
             for row in range(abs(SPEEDS[member][1])):
                 ysend[iy, offset + row] = read_rows(p_ref, member, leaving_row(member, row, ny))
 
+    for index in range(2):
+        for pair in range(nx // 2):
+            fold_z(index, pair)
+
+    def send_z():
+        for index in range(2):
+            z_copy(index).start()
+
+    pl.when(x_first)(send_z)
     pl.when(not_last)(meet_y)
     pl.when(jnp.logical_and(not_last, x_first))(tell_ready)
     for iy in range(2):
@@ -456,11 +477,7 @@
         meet_x()
         tell_plane()
 
-    for index in range(2):
-        for pair in range(nx // 2):
-            fold_z(index, pair)
-    for index in range(2):
-        z_copy(index).start()
+    pl.when(x_last)(send_z)
     pl.when(x_last)(tell_ready)
     for ix in range(2):
         for iz in range(2):
@@ -500,10 +517,9 @@
         z_copy(index).wait_recv()
         merge_z(index, lambda member, x: not travels(member, x))
     pl.when(first)(finish_edges)
-    for members in (TILTED, FLAT):
-        for ix, sign in enumerate(signs):
-            for member in members[sign]:
-                x_copy(ix, member).wait_send()
+    for group in range(3):
+        for ix in range(2):
+            x_group(ix, group).wait_send()
     for index in range(2):
         merge_z(index, travels)
     for iy, sign in enumerate(signs):
@@ -522,17 +538,17 @@
     for ix, sign in enumerate(signs):
         for iz in range(2):
             xz_copy(ix, iz).wait_recv()
+        x_group(ix, 0).wait_recv()
         for member in TILTED[sign]:
-            x_copy(ix, member).wait_recv()
             reach, iz = abs(SPEEDS[member][0]), 0 if SPEEDS[member][2] > 0 else 1
             for layer in range(reach):
                 half = 2 - reach + layer if sign > 0 else layer
                 for block in range(blocks):
                     target = halo[ix].at[XS[sign][member] + layer]
                     unfold(xzrecv[ix, iz], target, member, half, block, row_of(member, block))
-    for ix, sign in enumerate(signs):
-        for member in FLAT[sign]:
-            x_copy(ix, member).wait_recv()
+    for ix in range(2):
+        for group in (1, 2):
+            x_group(ix, group).wait_recv()
     for number, (sx, sy) in enumerate(CORNERS):
         ix = 0 if sx > 0 else 1
         d_copy(number).wait_recv()
@@ -620,7 +636,7 @@
             dma((2, 2, 2)),
             dma((2, 4)),
             dma((2, 4, 2)),
-            dma((2, 2, 11)),
+            dma((2, 2, 3)),
             pltpu.SemaphoreType.REGULAR,
             pltpu.SemaphoreType.REGULAR,
             pltpu.SemaphoreType.REGULAR((2,)),

time: 20.7 us -> 20 us (0.966)
  Pallas kernels: 20.6 us -> 19.8 us
    pallas_call x1, Pallas kernels: 18.2 us -> 17.4 us  [per_device(): pl.pallas_call(functools.partial(exchange_kernel, sizes), out_shape=(jax....]
where the time goes in v6:
time: 20 us; the launch traced here: 19.8 us
  Pallas kernels  19.8 us (99%)
    pallas_call x1, Pallas kernels, per_device(): pl.pallas_call(functools.partial(exchange_kernel, sizes), out_shape=(jax....  17.4 us
    pallas_call x1, Pallas kernels, per_device(): pl.pallas_call(functools.partial(emit_kernel, sizes), out_shape=jax.Shape...  2.4 us

profile of v6, /device:TPU:1, one launch (start us, length us, event | category | flops | bytes accessed | tf_op | source)
XLA Modules:
  0.0 19.8 jit_solution(13118730371993477081)
XLA Ops:
  0.0 17.4 %collide_exchange.1 = (f32[39,8,32,128]{3,2,1,0:T(8,128)S(1)}, f32[18,32,128]{2,1,0:T(8,128)S(1)}, f32[18,32,128]{2,1,0:T(8,128)S(1)}) custom-call(f32[39,8,24,128]{3,2,1,0:T(8,128)} %g_hbm.1, f32[8,24,128]{2,1,0:T(8,128)} %r_hbm.1), custom_call_target="tpu_custom_call" | custom-call | tf_op jit(solution)/shard_map/collide_exchange/pallas_call | solution.py:610
  17.4 2.4 %emit.1 = f32[39,8,24,128]{3,2,1,0:T(8,128)} custom-call(f32[39,8,32,128]{3,2,1,0:T(8,128)S(1)} %get-tuple-element.8.p_ref, f32[18,32,128]{2,1,0:T(8,128)S(1)} %get-tuple-element.9.up_ref, f32[18,32,128]{2,1,0:T(8,128)S(1)} %get-tuple-element.10.down_ref), custom_call_target="tpu_custom_call" | custom-call | tf_op jit(solution)/shard_map/emit/pallas_call | solution.py:649
